TPU v7x, 256 devices: a whole 4x4x8 slice. The times are simulated.
256 devices in a mesh: dp: 32 (over y, z), mp: 8 (over x, core).
Axes of the slice: x: 4, y: 4, z: 8, core: 2. Of those that a mesh axis runs over, the one named last changes fastest.
Arguments:
- grad_parts: bfloat16 [32, 8, 1024, 1024], P('dp', 'mp'), may hold values from -10 to 10
- left_stat: float32 [8, 1024, 1024], P('mp', 'dp'), may hold values from -60 to 500, as said below
- right_stat: float32 [8, 1024, 1024], P('mp', 'dp'), may hold values from -60 to 500, as said below
- left_root: bfloat16 [8, 1024, 1024], P('mp', 'dp'), may hold values from -2 to 2
- right_root: bfloat16 [8, 1024, 1024], P('mp', 'dp'), may hold values from -2 to 2
- due: int32 [8, 2], P('mp'), may hold values 0 or 1
Outputs:
- update: bfloat16 [8, 1024, 1024], P('mp')
- left_new: float32 [8, 1024, 1024], P('mp', 'dp')
- right_new: float32 [8, 1024, 1024], P('mp', 'dp')
- left_out: bfloat16 [8, 1024, 1024], P('mp', 'dp')
- right_out: bfloat16 [8, 1024, 1024], P('mp', 'dp')
Inputs may be any that keep to these rules, and one draw needn't show every extreme that they name: `left_stat`: every block is positive definite. `right_stat`: every block is positive definite. `due`: 1 where that statistic of the block gets a new root in this step.
All inputs are finite; a program needn't handle non-finite values.
Results may differ from a plain program's by a relative error of at most 0.022.
Values may be sent and summed in bfloat16 or wider, within the bound.
No kernel may reach another device: no remote copies, remote signals or barrier semaphores. Data moves between devices by JAX's collectives and lax.ppermute only.
A program may use at most 64 MiB of HBM per device.

v0:
```python
import functools

import jax
import jax.numpy as jnp
from jax import lax
from jax.experimental import pallas as pl
from jax.experimental.pallas import tpu as pltpu
from jax.sharding import Mesh
from jax.sharding import PartitionSpec as P

DP = ("y", "zh", "zl")
MP = ("x", "c")
WIDE = ("y", "zl")
NARROW = "zh"

epsilon = 1e-06
decay = 0.9


def dot(a, b, dims):
    return lax.dot_general(a, b, (dims, ((), ())), preferred_element_type=jnp.float32)


def exchange_sum(value, axes):
    groups = lax.axis_size(axes)
    parts = value.reshape(groups, value.shape[0] // groups, value.shape[1])
    parts = lax.all_to_all(parts, axes, 0, 0, tiled=True)
    return jnp.sum(parts.astype(jnp.float32), 0).astype(jnp.bfloat16)


def spread(value, axes):
    groups = lax.axis_size(axes)
    copies = jnp.broadcast_to(value[None], (groups, *value.shape))
    parts = lax.all_to_all(copies, axes, 0, 0, tiled=True)
    return parts.reshape(groups * value.shape[0], value.shape[1])


def choose_kernel(due, left_stat, right_stat, left_root, right_root, chosen):
    for k, stat, root in ((0, left_stat, left_root), (1, right_stat, right_root)):
        chosen[k] = jnp.where(due[0, k] == 1, stat[...].astype(jnp.bfloat16), root[...])


def choose(due, left_stat, right_stat, left_root, right_root):
    vector = pl.BlockSpec(memory_space=pltpu.VMEM)
    return pl.pallas_call(
        choose_kernel,
        out_shape=jax.ShapeDtypeStruct((2, *left_root.shape), jnp.bfloat16),
        in_specs=[pl.BlockSpec(memory_space=pltpu.SMEM), vector, vector, vector, vector],
        out_specs=vector,
        compiler_params=pltpu.CompilerParams(vmem_limit_bytes=4 * 2**20),
        name="choose",
    )(due, left_stat, right_stat, left_root, right_root)


def roots_kernel(tile, *refs):
    mean, due, place, grad, chosen, left_stat, right_stat = refs[:7]
    update, left_new, right_new, left_out, right_out = refs[7:12]
    picked, flipped, first, second, mixed, used, x, fourth, block, sems, sent = refs[12:]
    order = grad.shape[0]
    rows = left_stat.shape[0]
    weight = (1.0 - decay) / order
    columns = [slice(n * tile, (n + 1) * tile) for n in range(order // tile)]
    fetches = [
        pltpu.make_async_copy(chosen.at[k], picked.at[k], sems.at[k]) for k in range(2)
    ]
    for fetch in fetches:
        fetch.start()
    mine = pl.ds(pl.multiple_of(place[0], rows), rows)
    across = ((1,), (0,))
    factor = lax.rsqrt(jnp.full((1, 128), mean[0, 0] + epsilon, jnp.float32))
    factor = jnp.broadcast_to(factor[:, :1], (1, tile))

    def energy():
        total = jnp.zeros((128, order), jnp.float32)
        for i in range(0, order, 128):
            part = grad[i : i + 128, :].astype(jnp.float32)
            total = total + part * part
        return jnp.sum(total)

    squares = energy()

    def scale_of(k):
        row = lax.broadcasted_iota(jnp.int32, (128, 128), 0)
        col = lax.broadcasted_iota(jnp.int32, (128, 128), 1)
        diagonal = jnp.zeros((128, 128), jnp.float32)
        for i in range(0, order, 128):
            part = picked[k, i : i + 128, i : i + 128].astype(jnp.float32)
            diagonal = diagonal + jnp.where(row == col, part, 0.0)
        return (4.0 / order) * (decay * jnp.sum(diagonal) + weight * squares)

    def root_of(k, stat, new, out):
        scale_c = jnp.zeros((1, 128), jnp.float32)
        shrink = lift = None
        for n, cols in enumerate(columns):
            if k == 0:
                product = dot(grad[...], grad[cols, :], ((1,), (1,)))
            else:
                product = dot(flipped[...], grad[:, cols], across)
            if n == 0:
                fetches[k].wait()
                scale_c = scale_c + scale_of(k)
                shrink = jnp.broadcast_to((0.25 / scale_c)[:, :1], (1, tile))
                lift = 0.25 * jnp.exp(-0.25 * jnp.log(scale_c))
                lift = jnp.broadcast_to(lift[:, :1], (1, tile))
            block[:, cols] = product
            row = lax.broadcasted_iota(jnp.int32, (order, tile), 0)
            col = n * tile + lax.broadcasted_iota(jnp.int32, (order, tile), 1)
            statistic = decay * picked[k, :, cols].astype(jnp.float32) + weight * product
            first[:, cols] = (jnp.where(row == col, 1.25, 0.0) - statistic * shrink).astype(
                jnp.bfloat16
            )
        new[...] = stat[...] * decay + block[mine, :] * weight
        for cols in columns:
            square = dot(first[...], first[:, cols], across).astype(jnp.bfloat16)
            second[:, cols] = square
            mixed[:, cols] = (
                5.0 * first[:, cols].astype(jnp.float32) - 4.0 * square.astype(jnp.float32)
            ).astype(jnp.bfloat16)
            if k == 0:
                flipped[cols, :] = grad[:, cols].T
        for cols in columns:
            fourth[:, cols] = dot(second[...], second[:, cols], across).astype(jnp.bfloat16)
        for cols in columns:
            inner = dot(fourth[...], mixed[:, cols], across)
            root = lift * (5.0 * first[:, cols].astype(jnp.float32) - inner)
            used[:, cols] = jnp.where(
                due[0, k] == 1, root.astype(jnp.bfloat16), picked[k, :, cols]
            )
        out[...] = used[mine, :]

    root_of(0, left_stat, left_new, left_out)
    for cols in columns:
        x[:, cols] = dot(used[...], grad[:, cols], across).astype(jnp.bfloat16)
    root_of(1, right_stat, right_new, right_out)
    sends = []
    for n, cols in enumerate(columns):
        fourth[:, cols] = (dot(x[...], used[:, cols], across) * factor).astype(jnp.bfloat16)
        sends.append(
            pltpu.make_async_copy(fourth.at[:, cols], update.at[0, :, cols], sent.at[n])
        )
        sends[-1].start()
    for send in sends:
        send.wait()


def roots(mean, due, place, grad, chosen, left_stat, right_stat):
    order = grad.shape[0]
    tile = 512
    new = jax.ShapeDtypeStruct(left_stat.shape, jnp.float32)
    out = jax.ShapeDtypeStruct(left_stat.shape, jnp.bfloat16)
    scalar = pl.BlockSpec(memory_space=pltpu.SMEM)
    vector = pl.BlockSpec(memory_space=pltpu.VMEM)
    far = pl.BlockSpec(memory_space=pltpu.HBM)
    square = pltpu.VMEM((order, order), jnp.bfloat16)
    return pl.pallas_call(
        functools.partial(roots_kernel, tile),
        out_shape=(jax.ShapeDtypeStruct((1, order, order), jnp.bfloat16), new, new, out, out),
        in_specs=[scalar, scalar, scalar, vector, far, vector, vector],
        out_specs=(far, vector, vector, vector, vector),
        scratch_shapes=[
            pltpu.VMEM((2, order, order), jnp.bfloat16),
            *([square] * 7),
            pltpu.VMEM((order, order), jnp.float32),
            pltpu.SemaphoreType.DMA((2,)),
            pltpu.SemaphoreType.DMA((order // tile,)),
        ],
        cost_estimate=pl.CostEstimate(
            flops=10 * 2 * order**3, transcendentals=0, bytes_accessed=6 * 2**20
        ),
        compiler_params=pltpu.CompilerParams(vmem_limit_bytes=44 * 2**20),
        name="roots",
    )(mean, due, place, grad, chosen, left_stat, right_stat)


def per_device(grad_parts, left_stat, right_stat, left_root, right_root, due):
    row_count = left_stat.shape[1]
    row_start = lax.axis_index(DP) * row_count
    chosen = choose(due, left_stat[0], right_stat[0], left_root[0], right_root[0])
    chosen = lax.all_gather(chosen, DP, axis=1, tiled=True)
    chosen = pltpu.with_memory_space_constraint(chosen, pltpu.HBM)

    rows = exchange_sum(exchange_sum(grad_parts[0, 0], WIDE), NARROW)
    chunk = spread(rows, NARROW)
    squares = jnp.sum(rows.astype(jnp.float32) ** 2)
    squares = lax.psum(squares, (*DP, *MP))
    grad = spread(chunk, WIDE)
    place = row_start.astype(jnp.int32).reshape(1)
    update, left_new, right_new, left_out, right_out = refs[7:12]
    picked, flipped, first, second, mixed, used, x, fourth, block, sems, sent = refs[12:]
    order = grad.shape[0]
    rows = left_stat.shape[0]
    weight = (1.0 - decay) / order
    columns = [slice(n * tile, (n + 1) * tile) for n in range(order // tile)]
    fetches = [
        pltpu.make_async_copy(chosen.at[k], picked.at[k], sems.at[k]) for k in range(2)
    ]
    for fetch in fetches:
        fetch.start()
    mine = pl.ds(pl.multiple_of(place[0], rows), rows)
    across = ((1,), (0,))
    block_squares = jnp.sum(sums[:, place[1]], 0)[:1]
    squares = jnp.sum(jnp.sum(sums[...], 0), 0)[:1]
    count = float(sums.shape[1] * order * order)
    factor = jnp.broadcast_to(lax.rsqrt(squares / count + epsilon)[:, :1], (1, tile))

    def scale_of(k):
        row = lax.broadcasted_iota(jnp.int32, (128, 128), 0)
        col = lax.broadcasted_iota(jnp.int32, (128, 128), 1)
        diagonal = jnp.zeros((128, 128), jnp.float32)
        for i in range(0, order, 128):
            part = picked[k, i : i + 128, i : i + 128].astype(jnp.float32)
            diagonal = diagonal + jnp.where(row == col, part, 0.0)
        return (4.0 / order) * (decay * jnp.sum(diagonal) + weight * squares)

    def root_of(k, stat, new, out):
        scale_c = jnp.zeros((1, 128), jnp.float32)
        shrink = lift = None
        for n, cols in enumerate(columns):
            if k == 0:
                product = dot(grad[...], grad[cols, :], ((1,), (1,)))
            else:
                product = dot(flipped[...], grad[:, cols], across)
            if n == 0:
                fetches[k].wait()
                scale_c = scale_c + scale_of(k)
                shrink = jnp.broadcast_to((0.25 / scale_c)[:, :1], (1, tile))
                lift = 0.25 * jnp.exp(-0.25 * jnp.log(scale_c))
                lift = jnp.broadcast_to(lift[:, :1], (1, tile))
            block[:, cols] = product
            row = lax.broadcasted_iota(jnp.int32, (order, tile), 0)
            col = n * tile + lax.broadcasted_iota(jnp.int32, (order, tile), 1)
            statistic = decay * picked[k, :, cols].astype(jnp.float32) + weight * product
            first[:, cols] = (jnp.where(row == col, 1.25, 0.0) - statistic * shrink).astype(
                jnp.bfloat16
            )
        new[...] = stat[...] * decay + block[mine, :] * weight
        for cols in columns:
            square = dot(first[...], first[:, cols], across).astype(jnp.bfloat16)
            second[:, cols] = square
            mixed[:, cols] = (
                5.0 * first[:, cols].astype(jnp.float32) - 4.0 * square.astype(jnp.float32)
            ).astype(jnp.bfloat16)
            if k == 0:
                flipped[cols, :] = grad[:, cols].T
        for cols in columns:
            fourth[:, cols] = dot(second[...], second[:, cols], across).astype(jnp.bfloat16)
        for cols in columns:
            inner = dot(fourth[...], mixed[:, cols], across)
            root = lift * (5.0 * first[:, cols].astype(jnp.float32) - inner)
            used[:, cols] = jnp.where(
                due[0, k] == 1, root.astype(jnp.bfloat16), picked[k, :, cols]
            )
        out[...] = used[mine, :]

    root_of(0, left_stat, left_new, left_out)
    for cols in columns:
        x[:, cols] = dot(used[...], grad[:, cols], across).astype(jnp.bfloat16)
    root_of(1, right_stat, right_new, right_out)
    sends = []
    for n, cols in enumerate(columns):
        fourth[:, cols] = (dot(x[...], used[:, cols], across) * factor).astype(jnp.bfloat16)
        sends.append(
            pltpu.make_async_copy(fourth.at[:, cols], update.at[0, :, cols], sent.at[n])
        )
        sends[-1].start()
    for send in sends:
        send.wait()


def roots(mean, due, place, grad, chosen, left_stat, right_stat):
    order = grad.shape[0]
    tile = 512
    new = jax.ShapeDtypeStruct(left_stat.shape, jnp.float32)
    out = jax.ShapeDtypeStruct(left_stat.shape, jnp.bfloat16)
    scalar = pl.BlockSpec(memory_space=pltpu.SMEM)
    vector = pl.BlockSpec(memory_space=pltpu.VMEM)
    far = pl.BlockSpec(memory_space=pltpu.HBM)
    square = pltpu.VMEM((order, order), jnp.bfloat16)
    return pl.pallas_call(
        functools.partial(roots_kernel, tile),
        out_shape=(jax.ShapeDtypeStruct((1, order, order), jnp.bfloat16), new, new, out, out),
        in_specs=[scalar, scalar, scalar, vector, far, vector, vector],
        out_specs=(far, vector, vector, vector, vector),
        scratch_shapes=[
            pltpu.VMEM((2, order, order), jnp.bfloat16),
            *([square] * 7),
            pltpu.VMEM((order, order), jnp.float32),
            pltpu.SemaphoreType.DMA((2,)),
            pltpu.SemaphoreType.DMA((order // tile,)),
        ],
        cost_estimate=pl.CostEstimate(
            flops=10 * 2 * order**3, transcendentals=0, bytes_accessed=6 * 2**20
        ),
        compiler_params=pltpu.CompilerParams(vmem_limit_bytes=44 * 2**20),
        name="roots",
    )(mean, due, place, grad, chosen, left_stat, right_stat)


def per_device(grad_parts, left_stat, right_stat, left_root, right_root, due):
    row_count = left_stat.shape[1]
    row_start = lax.axis_index(DP) * row_count
    chosen = choose(due, left_stat[0], right_stat[0], left_root[0], right_root[0])
    chosen = lax.all_gather(chosen, DP, axis=1, tiled=True)
    chosen = pltpu.with_memory_space_constraint(chosen, pltpu.HBM)

    rows = exchange_sum(exchange_sum(grad_parts[0, 0], WIDE), NARROW)
    chunk = spread(rows, NARROW)
    squares = jnp.sum(rows.astype(jnp.float32) ** 2)
    squares = lax.psum(squares, (*DP, *MP))
    mean = squares / float(lax.axis_size(MP) * left_stat.shape[-1] ** 2)
    grad = spread(chunk, WIDE)
    mean = mean.reshape(1, 1)
    place = jnp.stack([row_start, lax.axis_index(MP)]).astype(jnp.int32)
    update, left_new, right_new, left_out, right_out = roots(
        mean, due, place, grad, chosen, left_stat[0], right_stat[0]
    )
    return (update, left_new[None], right_new[None], left_out[None], right_out[None])


def solution(mesh):
    torus = Mesh(mesh.devices.reshape(4, 4, 2, 4, 2), ("y", "zh", "zl", "x", "c"))
    in_specs = (
        P(DP, MP, None, None),
        P(MP, DP, None),
        P(MP, DP, None),
        P(MP, DP, None),
        P(MP, DP, None),
        P(MP, None),
    )
    out_specs = (
        P(MP, None, None),
        P(MP, DP, None),
        P(MP, DP, None),
        P(MP, DP, None),
        P(MP, DP, None),
    )
    return jax.shard_map(
        per_device, mesh=torus, in_specs=in_specs, out_specs=out_specs, check_vma=False
    )
```

profile of v0, /device:TPU:2, one launch (start us, length us, event | category | flops | bytes accessed | tf_op | source)
XLA Modules:
  0.0 212.6 jit_solution(5585370730496230530)
XLA Ops:
  7.2 0.0 copy-start
  7.2 0.0 copy-start.1
  7.2 0.0 copy-start.2
  7.2 0.0 copy-start.3
  7.2 0.0 copy-start.4
  7.2 6.0 %all-to-all-start = ((bf16[8,128,1024]{2,1,0:T(8,128)(2,1)}), bf16[8,128,1024]{2,1,0:T(8,128)(2,1)}, u32[]{:S(2)}, u32[]{:S(2)}) async-start(bf16[8,128,1024]{2,1,0:T(8,128)(2,1)} %bitcast.22), calls=%async_computation | async-start | bytes 4194304 | tf_op jit(solution)/shard_map/all_to_all | solution.py:27
  13.2 0.0 all-gather.2.cloned.1.call-start
  13.2 0.0 copy-done
  13.2 0.0 copy-done.1
  13.2 0.0 copy-done.2
  13.3 0.0 copy-done.3
  13.3 0.0 copy-done.4
  13.3 1.2 choose.1
  14.5 0.0 all-gather.2.cloned.1.call-update
  14.5 27.0 %all-to-all-done = bf16[8,128,1024]{2,1,0:T(8,128)(2,1)} async-done(((bf16[8,128,1024]{2,1,0:T(8,128)(2,1)}), bf16[8,128,1024]{2,1,0:T(8,128)(2,1)}, u32[]{:S(2)}, u32[]{:S(2)}) %all-to-all-start) | async-done | bytes 2097184 | tf_op jit(solution)/shard_map/all_to_all | solution.py:27
  41.5 2.0 reduce_sum.33
  43.5 18.9 %all_to_all.20 = bf16[4,32,1024]{2,1,0:T(8,128)(2,1)S(1)} all-to-all(bf16[4,32,1024]{2,1,0:T(8,128)(2,1)S(1)} %bitcast.23), channel_id=1, replica_groups=mesh['y'=4,'zh'=4,'zl'=2,'x'=4,'c'=2] {'zh'}, dimensions={0} | all-to-all | bytes 524288 | tf_op jit(solution)/shard_map/all_to_all | solution.py:27
  62.5 11.8 %all_to_all.21 = bf16[4,32,1024]{2,1,0:T(8,128)(2,1)S(1)} all-to-all(bf16[4,32,1024]{2,1,0:T(8,128)(2,1)S(1)} %broadcast_in_dim.25), channel_id=1, replica_groups=mesh['y'=4,'zh'=4,'zl'=2,'x'=4,'c'=2] {'zh'}, dimensions={0} | all-to-all | bytes 524288 | tf_op jit(solution)/shard_map/all_to_all | solution.py:34
  74.3 1.6 broadcast_in_dim.27
  75.9 4.7 %all-to-all-start.3 = ((bf16[8,128,1024]{2,1,0:T(8,128)(2,1)}), bf16[8,128,1024]{2,1,0:T(8,128)(2,1)S(1)}, u32[]{:S(2)}, u32[]{:S(2)}) async-start(bf16[8,128,1024]{2,1,0:T(8,128)(2,1)} %broadcast_in_dim.27), calls=%async_computation.3 | async-start | bytes 4194304 | tf_op jit(solution)/shard_map/all_to_all | solution.py:34
  80.6 0.6 multiply_reduce_fusion
  81.2 0.1 pad_add_fusion.refs_2_
  81.3 97.5 %psum.7 = f32[]{:T(128)} all-reduce(f32[]{:T(128)} %multiply_reduce_fusion), channel_id=1, replica_groups=mesh['y'=4,'zh'=4,'zl'=2,'x'=4,'c'=2] {'y','zh','zl','x','c'}, use_global_device_ids=true, to_apply=%region_3.0 | all-reduce | flops 1 | bytes 8 | tf_op jit(solution)/shard_map/psum | solution.py:309
  179.4 0.0 all-gather.2.cloned.1.call-done.refs_4_
  179.4 0.0 all-to-all-done.3
  179.5 26.3 %roots.1 = (bf16[1,1024,1024]{2,1,0:T(8,128)(2,1)}, f32[32,1024]{1,0:T(8,128)}, f32[32,1024]{1,0:T(8,128)}, bf16[32,1024]{1,0:T(8,128)(2,1)}, bf16[32,1024]{1,0:T(8,128)(2,1)}) custom-call(f32[1,1]{1,0:T(1,128)} %bitcast.2.refs_0_, s32[1,2]{1,0:T(1,128)S(1)} %copy-done.4, s32[2]{0:T(128)S(1)} %pad_add_fusion.refs_2_, bf16[1024,1024]{1,0:T(8,128)(2,1)S(1)} %bitcast.15, ...), custom_call_target="tpu_custom_call" | custom-call | flops 21474836480 | bytes 6291456 | tf_op jit(solution)/shard_map/roots/pallas_call | solution.py:279
  (2 shorter events, 0.1 us)
Async XLA Ops:
  7.2 6.1 %copy-start = (f32[1,32,1024]{2,1,0:T(8,128)S(1)}, f32[1,32,1024]{2,1,0:T(8,128)}, u32[]{:S(2)}) copy-start(f32[1,32,1024]{2,1,0:T(8,128)} %param.7) | copy-start | bytes 393220
  7.2 6.1 %copy-start.1 = (f32[1,32,1024]{2,1,0:T(8,128)S(1)}, f32[1,32,1024]{2,1,0:T(8,128)}, u32[]{:S(2)}) copy-start(f32[1,32,1024]{2,1,0:T(8,128)} %param.8) | copy-start | bytes 393220
  7.2 6.1 %copy-start.2 = (bf16[1,32,1024]{2,1,0:T(8,128)(2,1)S(1)}, bf16[1,32,1024]{2,1,0:T(8,128)(2,1)}, u32[]{:S(2)}) copy-start(bf16[1,32,1024]{2,1,0:T(8,128)(2,1)} %param.9) | copy-start | bytes 196612
  7.2 6.1 %copy-start.3 = (bf16[1,32,1024]{2,1,0:T(8,128)(2,1)S(1)}, bf16[1,32,1024]{2,1,0:T(8,128)(2,1)}, u32[]{:S(2)}) copy-start(bf16[1,32,1024]{2,1,0:T(8,128)(2,1)} %param.10) | copy-start | bytes 196612
  7.2 6.1 %copy-start.4 = (s32[1,2]{1,0:T(1,128)S(1)}, s32[1,2]{1,0:T(1,128)}, u32[]{:S(2)}) copy-start(s32[1,2]{1,0:T(1,128)} %refs_1_.1) | copy-start | bytes 28
  7.2 34.3 %all-to-all-start = ((bf16[8,128,1024]{2,1,0:T(8,128)(2,1)}), bf16[8,128,1024]{2,1,0:T(8,128)(2,1)}, u32[]{:S(2)}, u32[]{:S(2)}) async-start(bf16[8,128,1024]{2,1,0:T(8,128)(2,1)} %bitcast.22), calls=%async_computation | async-start | bytes 4194304 | tf_op jit(solution)/shard_map/all_to_all | solution.py:27
  13.2 166.2 %all-gather.2.cloned.1.call-start = ((), (), s32[]{:S(2)}) async-start(), calls=%async_computation.4 | async-start | bytes 4325376 | tf_op jit(solution)/shard_map/all_gather | solution.py:303
  75.9 103.6 %all-to-all-start.3 = ((bf16[8,128,1024]{2,1,0:T(8,128)(2,1)}), bf16[8,128,1024]{2,1,0:T(8,128)(2,1)S(1)}, u32[]{:S(2)}, u32[]{:S(2)}) async-start(bf16[8,128,1024]{2,1,0:T(8,128)(2,1)} %broadcast_in_dim.27), calls=%async_computation.3 | async-start | bytes 4194304 | tf_op jit(solution)/shard_map/all_to_all | solution.py:34
Sparse Core Ops, SparseCore 0:
  17.2 102.0 all-gather.1
where the time goes:
time: 216 us; the launch traced here: 213 us
  blocking collectives  128 us (59%)
  Pallas kernels  27.5 us (13%)
  waiting for transfers between devices  27.1 us (13%)
  between operations  14.8 us (7%)
  starting transfers between devices  10.7 us (5%)
  other arithmetic  2.71 us (1%)
    psum x1, blocking collectives, per_device(): squares = lax.psum(squares, (*DP, *MP))  97.5 us
    all_to_all x1, waiting for transfers between devices, exchange_sum(): parts = lax.all_to_all(parts, axes, 0, 0, tiled=True)  27 us
    pallas_call x1, Pallas kernels, roots(): pl.pallas_call(functools.partial(roots_kernel, tile), out_shape=(jax.Shap...  26.3 us
    all_to_all x1, blocking collectives, exchange_sum(): parts = lax.all_to_all(parts, axes, 0, 0, tiled=True)  18.9 us
    all_to_all x1, blocking collectives, spread(): parts = lax.all_to_all(copies, axes, 0, 0, tiled=True)  11.8 us
    all_to_all x1, starting transfers between devices, exchange_sum(): parts = lax.all_to_all(parts, axes, 0, 0, tiled=True)  5.97 us
    all_to_all x1, starting transfers between devices, spread(): parts = lax.all_to_all(copies, axes, 0, 0, tiled=True)  4.7 us
  transfers between devices with their start and end apart: 3, of which 1 were waited for; matrix products, arithmetic and copies ran while one was open for 2% of the time, Pallas kernels for 1%

commit v1 on v0

v1 whole, which is shorter than its diff:
```python
import functools

import jax
import jax.numpy as jnp
from jax import lax
from jax.experimental import pallas as pl
from jax.experimental.pallas import tpu as pltpu
from jax.sharding import Mesh
from jax.sharding import PartitionSpec as P

DP = ("y", "zh", "zl")
MP = ("x", "c")
WIDE = ("y", "zl")
NARROW = "zh"

epsilon = 1e-06
decay = 0.9


def dot(a, b, dims):
    return lax.dot_general(a, b, (dims, ((), ())), preferred_element_type=jnp.float32)


def exchange_sum(value, axes):
    groups = lax.axis_size(axes)
    parts = value.reshape(groups, value.shape[0] // groups, value.shape[1])
    parts = lax.all_to_all(parts, axes, 0, 0, tiled=True)
    return jnp.sum(parts.astype(jnp.float32), 0).astype(jnp.bfloat16)


def spread(value, axes):
    groups = lax.axis_size(axes)
    copies = jnp.broadcast_to(value[None], (groups, *value.shape))
    parts = lax.all_to_all(copies, axes, 0, 0, tiled=True)
    return parts.reshape(groups * value.shape[0], value.shape[1])


def sum_of_four(value, axes):
    others = []
    for mask in (1, 2, 3):
        swap = [(i, i ^ mask) for i in range(4)]
        others.append(lax.ppermute(value, axes, swap))
    return (value + others[0]) + (others[1] + others[2])


def choose_kernel(due, left_stat, right_stat, left_root, right_root, chosen):
    for k, stat, root in ((0, left_stat, left_root), (1, right_stat, right_root)):
        chosen[k] = jnp.where(due[0, k] == 1, stat[...].astype(jnp.bfloat16), root[...])


def choose(due, left_stat, right_stat, left_root, right_root):
    vector = pl.BlockSpec(memory_space=pltpu.VMEM)
    return pl.pallas_call(
        choose_kernel,
        out_shape=jax.ShapeDtypeStruct((2, *left_root.shape), jnp.bfloat16),
        in_specs=[pl.BlockSpec(memory_space=pltpu.SMEM), vector, vector, vector, vector],
        out_specs=vector,
        compiler_params=pltpu.CompilerParams(vmem_limit_bytes=4 * 2**20),
        name="choose",
    )(due, left_stat, right_stat, left_root, right_root)


def roots_kernel(tile, blocks, *refs):
    total, due, place, grad, chosen, left_stat, right_stat = refs[:7]
    update, left_new, right_new, left_out, right_out = refs[7:12]
    picked, flipped, first, second, mixed, used, x, fourth, block, sems, sent = refs[12:]
    order = grad.shape[0]
    rows = left_stat.shape[0]
    weight = (1.0 - decay) / order
    columns = [slice(n * tile, (n + 1) * tile) for n in range(order // tile)]
    fetches = [
        pltpu.make_async_copy(chosen.at[k], picked.at[k], sems.at[k]) for k in range(2)
    ]
    for fetch in fetches:
        fetch.start()
    mine = pl.ds(pl.multiple_of(place[0], rows), rows)
    across = ((1,), (0,))
    factor = lax.rsqrt(total[:1] / float(blocks * order * order) + epsilon)
    factor = jnp.broadcast_to(factor[:, :1], (1, tile))

    def energy():
        partial = jnp.zeros((128, order), jnp.float32)
        for i in range(0, order, 128):
            part = grad[i : i + 128, :].astype(jnp.float32)
            partial = partial + part * part
        return jnp.sum(partial)

    squares = energy()

    def scale_of(k):
        row = lax.broadcasted_iota(jnp.int32, (128, 128), 0)
        col = lax.broadcasted_iota(jnp.int32, (128, 128), 1)
        diagonal = jnp.zeros((128, 128), jnp.float32)
        for i in range(0, order, 128):
            part = picked[k, i : i + 128, i : i + 128].astype(jnp.float32)
            diagonal = diagonal + jnp.where(row == col, part, 0.0)
        return (4.0 / order) * (decay * jnp.sum(diagonal) + weight * squares)

    def root_of(k, stat, new, out):
        scale_c = jnp.zeros((1, 128), jnp.float32)
        shrink = lift = None
        for n, cols in enumerate(columns):
            if k == 0:
                product = dot(grad[...], grad[cols, :], ((1,), (1,)))
            else:
                product = dot(flipped[...], grad[:, cols], across)
            if n == 0:
                fetches[k].wait()
                scale_c = scale_c + scale_of(k)
                shrink = jnp.broadcast_to((0.25 / scale_c)[:, :1], (1, tile))
                lift = 0.25 * jnp.exp(-0.25 * jnp.log(scale_c))
                lift = jnp.broadcast_to(lift[:, :1], (1, tile))
            block[:, cols] = product
            row = lax.broadcasted_iota(jnp.int32, (order, tile), 0)
            col = n * tile + lax.broadcasted_iota(jnp.int32, (order, tile), 1)
            statistic = decay * picked[k, :, cols].astype(jnp.float32) + weight * product
            first[:, cols] = (jnp.where(row == col, 1.25, 0.0) - statistic * shrink).astype(
                jnp.bfloat16
            )
        new[...] = stat[...] * decay + block[mine, :] * weight
        for cols in columns:
            square = dot(first[...], first[:, cols], across).astype(jnp.bfloat16)
            second[:, cols] = square
            mixed[:, cols] = (
                5.0 * first[:, cols].astype(jnp.float32) - 4.0 * square.astype(jnp.float32)
            ).astype(jnp.bfloat16)
            if k == 0:
                flipped[cols, :] = grad[:, cols].T
        for cols in columns:
            fourth[:, cols] = dot(second[...], second[:, cols], across).astype(jnp.bfloat16)
        for cols in columns:
            inner = dot(fourth[...], mixed[:, cols], across)
            root = lift * (5.0 * first[:, cols].astype(jnp.float32) - inner)
            used[:, cols] = jnp.where(
                due[0, k] == 1, root.astype(jnp.bfloat16), picked[k, :, cols]
            )
        out[...] = used[mine, :]

    root_of(0, left_stat, left_new, left_out)
    for cols in columns:
        x[:, cols] = dot(used[...], grad[:, cols], across).astype(jnp.bfloat16)
    root_of(1, right_stat, right_new, right_out)
    sends = []
    for n, cols in enumerate(columns):
        fourth[:, cols] = (dot(x[...], used[:, cols], across) * factor).astype(jnp.bfloat16)
        sends.append(
            pltpu.make_async_copy(fourth.at[:, cols], update.at[0, :, cols], sent.at[n])
        )
        sends[-1].start()
    for send in sends:
        send.wait()


def roots(total, due, place, grad, chosen, left_stat, right_stat):
    order = grad.shape[0]
    tile = 512
    new = jax.ShapeDtypeStruct(left_stat.shape, jnp.float32)
    out = jax.ShapeDtypeStruct(left_stat.shape, jnp.bfloat16)
    scalar = pl.BlockSpec(memory_space=pltpu.SMEM)
    vector = pl.BlockSpec(memory_space=pltpu.VMEM)
    far = pl.BlockSpec(memory_space=pltpu.HBM)
    square = pltpu.VMEM((order, order), jnp.bfloat16)
    return pl.pallas_call(
        functools.partial(roots_kernel, tile, lax.axis_size(MP)),
        out_shape=(jax.ShapeDtypeStruct((1, order, order), jnp.bfloat16), new, new, out, out),
        in_specs=[vector, scalar, scalar, vector, far, vector, vector],
        out_specs=(far, vector, vector, vector, vector),
        scratch_shapes=[
            pltpu.VMEM((2, order, order), jnp.bfloat16),
            *([square] * 7),
            pltpu.VMEM((order, order), jnp.float32),
            pltpu.SemaphoreType.DMA((2,)),
            pltpu.SemaphoreType.DMA((order // tile,)),
        ],
        cost_estimate=pl.CostEstimate(
            flops=10 * 2 * order**3, transcendentals=0, bytes_accessed=6 * 2**20
        ),
        compiler_params=pltpu.CompilerParams(vmem_limit_bytes=44 * 2**20),
        name="roots",
    )(total, due, place, grad, chosen, left_stat, right_stat)


def per_device(grad_parts, left_stat, right_stat, left_root, right_root, due):
    row_count = left_stat.shape[1]
    row_start = lax.axis_index(DP) * row_count
    chosen = choose(due, left_stat[0], right_stat[0], left_root[0], right_root[0])
    chosen = lax.all_gather(chosen, DP, axis=1, tiled=True)
    chosen = pltpu.with_memory_space_constraint(chosen, pltpu.HBM)

    rows = exchange_sum(exchange_sum(grad_parts[0, 0], WIDE), NARROW)
    chunk = spread(rows, NARROW)
    squares = jnp.sum(chunk.astype(jnp.float32) ** 2)
    total = jnp.full((8, 128), squares, jnp.float32)
    for axes in (("zl", "c"), ("x",), ("y",)):
        total = sum_of_four(total, axes)
    grad = spread(chunk, WIDE)
    place = row_start.astype(jnp.int32).reshape(1)
    update, left_new, right_new, left_out, right_out = roots(
        total, due, place, grad, chosen, left_stat[0], right_stat[0]
    )
    return (update, left_new[None], right_new[None], left_out[None], right_out[None])


def solution(mesh):
    torus = Mesh(mesh.devices.reshape(4, 4, 2, 4, 2), ("y", "zh", "zl", "x", "c"))
    in_specs = (
        P(DP, MP, None, None),
        P(MP, DP, None),
        P(MP, DP, None),
        P(MP, DP, None),
        P(MP, DP, None),
        P(MP, None),
    )
    out_specs = (
        P(MP, None, None),
        P(MP, DP, None),
        P(MP, DP, None),
        P(MP, DP, None),
        P(MP, DP, None),
    )
    return jax.shard_map(
        per_device, mesh=torus, in_specs=in_specs, out_specs=out_specs, check_vma=False
    )
```

time: 216 us -> 166 us (0.77)
  blocking collectives: 128 us -> 30.7 us
  waiting for transfers between devices: 27.1 us -> 65.2 us
  starting transfers between devices: 10.7 us -> 21.4 us
    psum x1 -> x0, blocking collectives: 97.5 us -> none  [per_device(): squares = lax.psum(squares, (*DP, *MP))]
    ppermute x0 -> x9, waiting for transfers between devices: none -> 38.2 us  [sum_of_four(): others.append(lax.ppermute(value, axes, swap))]
    ppermute x0 -> x9, starting transfers between devices: none -> 10.7 us  [sum_of_four(): others.append(lax.ppermute(value, axes, swap))]
  transfers between devices with their start and end apart: 3 -> 12, of which waited for: 1 -> 5; matrix products, arithmetic and copies ran while one was open for 2% -> 3% of each run, Pallas kernels for 1% -> 1%
where the time goes in v1:
time: 166 us; the launch traced here: 165 us
  waiting for transfers between devices  65.2 us (39%)
  blocking collectives  30.7 us (18%)
  Pallas kernels  27.5 us (17%)
  starting transfers between devices  21.4 us (13%)
  between operations  14.2 us (9%)
  other arithmetic  3.4 us (2%)
  local copies, waits for them, and re-layouts  2.27 us (1%)
    ppermute x9, waiting for transfers between devices, sum_of_four(): others.append(lax.ppermute(value, axes, swap))  38.2 us
    all_to_all x1, waiting for transfers between devices, exchange_sum(): parts = lax.all_to_all(parts, axes, 0, 0, tiled=True)  27 us
    pallas_call x1, Pallas kernels, roots(): pl.pallas_call(functools.partial(roots_kernel, tile, lax.axis_size(MP)),...  26.3 us
    all_to_all x1, blocking collectives, exchange_sum(): parts = lax.all_to_all(parts, axes, 0, 0, tiled=True)  18.9 us
    all_to_all x1, blocking collectives, spread(): parts = lax.all_to_all(copies, axes, 0, 0, tiled=True)  11.8 us
    ppermute x9, starting transfers between devices, sum_of_four(): others.append(lax.ppermute(value, axes, swap))  10.7 us
    all_to_all x1, starting transfers between devices, exchange_sum(): parts = lax.all_to_all(parts, axes, 0, 0, tiled=True)  5.97 us
    all_to_all x1, starting transfers between devices, spread(): parts = lax.all_to_all(copies, axes, 0, 0, tiled=True)  4.7 us
  transfers between devices with their start and end apart: 12, of which 5 were waited for; matrix products, arithmetic and copies ran while one was open for 3% of the time, Pallas kernels for 1%

profile of v1, /device:TPU:2, one launch (start us, length us, event | category | flops | bytes accessed | tf_op | source)
XLA Modules:
  0.0 164.7 jit_solution(15142913427365953234)
XLA Ops:
  7.2 0.0 copy-start
  7.2 0.0 copy-start.1
  7.2 0.0 copy-start.2
  7.2 0.0 copy-start.3
  7.2 0.0 copy-start.4
  7.2 6.0 %all-to-all-start = ((bf16[8,128,1024]{2,1,0:T(8,128)(2,1)}), bf16[8,128,1024]{2,1,0:T(8,128)(2,1)}, u32[]{:S(2)}, u32[]{:S(2)}) async-start(bf16[8,128,1024]{2,1,0:T(8,128)(2,1)} %bitcast.21), calls=%async_computation | async-start | bytes 4194304 | tf_op jit(solution)/shard_map/all_to_all | solution.py:27
  13.2 0.0 all-gather.2.cloned.1.call-start
  13.2 0.0 copy-done
  13.2 0.0 copy-done.1
  13.2 0.0 copy-done.2
  13.3 0.0 copy-done.3
  13.3 0.0 copy-done.4
  13.3 1.2 choose.1
  14.5 0.0 all-gather.2.cloned.1.call-update
  14.5 27.0 %all-to-all-done = bf16[8,128,1024]{2,1,0:T(8,128)(2,1)} async-done(((bf16[8,128,1024]{2,1,0:T(8,128)(2,1)}), bf16[8,128,1024]{2,1,0:T(8,128)(2,1)}, u32[]{:S(2)}, u32[]{:S(2)}) %all-to-all-start) | async-done | bytes 2097184 | tf_op jit(solution)/shard_map/all_to_all | solution.py:27
  41.5 2.0 %reduce_sum.33 = bf16[128,1024]{1,0:T(8,128)(2,1)S(1)} reduce(bf16[8,128,1024]{2,1,0:T(8,128)(2,1)} %all-to-all-done, bf16[]{:T(256)} %constant.8.clone.1), dimensions={0}, to_apply=%region_0.0 | reduce | flops 917504 | bytes 2359298 | tf_op jit(solution)/shard_map/reduce_sum | solution.py:28
  43.5 18.9 %all_to_all.20 = bf16[4,32,1024]{2,1,0:T(8,128)(2,1)S(1)} all-to-all(bf16[4,32,1024]{2,1,0:T(8,128)(2,1)S(1)} %bitcast.22), channel_id=1, replica_groups=mesh['y'=4,'zh'=4,'zl'=2,'x'=4,'c'=2] {'zh'}, dimensions={0} | all-to-all | bytes 524288 | tf_op jit(solution)/shard_map/all_to_all | solution.py:27
  62.5 11.8 %all_to_all.21 = bf16[4,32,1024]{2,1,0:T(8,128)(2,1)S(1)} all-to-all(bf16[4,32,1024]{2,1,0:T(8,128)(2,1)S(1)} %broadcast_in_dim.28), channel_id=1, replica_groups=mesh['y'=4,'zh'=4,'zl'=2,'x'=4,'c'=2] {'zh'}, dimensions={0} | all-to-all | bytes 524288 | tf_op jit(solution)/shard_map/all_to_all | solution.py:34
  74.3 1.6 broadcast_in_dim.31
  75.9 4.7 %all-to-all-start.3 = ((bf16[8,128,1024]{2,1,0:T(8,128)(2,1)}), bf16[8,128,1024]{2,1,0:T(8,128)(2,1)S(1)}, u32[]{:S(2)}, u32[]{:S(2)}) async-start(bf16[8,128,1024]{2,1,0:T(8,128)(2,1)} %broadcast_in_dim.31), calls=%async_computation.3 | async-start | bytes 4194304 | tf_op jit(solution)/shard_map/all_to_all | solution.py:34
  80.6 0.7 multiply_reduce_fusion
  81.3 0.6 broadcast_in_dim.29
  82.0 2.1 %collective-permute-start.1 = (f32[8,128]{1,0:T(8,128)S(1)}, f32[8,128]{1,0:T(8,128)S(1)}, u32[]{:S(2)}, u32[]{:S(2)}) collective-permute-start(f32[8,128]{1,0:T(8,128)S(1)} %broadcast_in_dim.29), channel_id=1, source_target_pairs={{0,8},{1,9},{8,0},{9,1},{2,10},{3,11},{10,2},{11,3},{4,12},{5,13},... | collective-permute-start | bytes 12296 | tf_op jit(solution)/shard_map/ppermute | solution.py:42
  84.1 0.0 collective-permute-start.2
  84.1 0.2 collective-permute-start
  84.3 32.7 %collective-permute-done.1 = f32[8,128]{1,0:T(8,128)S(1)} collective-permute-done((f32[8,128]{1,0:T(8,128)S(1)}, f32[8,128]{1,0:T(8,128)S(1)}, u32[]{:S(2)}, u32[]{:S(2)}) %collective-permute-start.1) | collective-permute-done | bytes 4128 | tf_op jit(solution)/shard_map/ppermute | solution.py:42
  117.0 0.0 collective-permute-done.2
  117.0 0.0 collective-permute-done
  117.0 0.7 add_add_fusion.2
  117.7 1.9 %collective-permute-start.5 = (f32[8,128]{1,0:T(8,128)S(1)}, f32[8,128]{1,0:T(8,128)S(1)}, u32[]{:S(2)}, u32[]{:S(2)}) collective-permute-start(f32[8,128]{1,0:T(8,128)S(1)} %add_add_fusion.2), channel_id=1, source_target_pairs={{0,6},{2,4},{4,2},{6,0},{1,7},{3,5},{5,3},{7,1},{8,14},{10,12},{12... | collective-permute-start | bytes 12296 | tf_op jit(solution)/shard_map/ppermute | solution.py:42
  119.5 0.8 collective-permute-start.4
  120.4 1.5 collective-permute-start.3
  121.8 0.0 collective-permute-done.5
  121.9 2.8 %collective-permute-done.4 = f32[8,128]{1,0:T(8,128)S(1)} collective-permute-done((f32[8,128]{1,0:T(8,128)S(1)}, f32[8,128]{1,0:T(8,128)S(1)}, u32[]{:S(2)}, u32[]{:S(2)}) %collective-permute-start.4) | collective-permute-done | bytes 4128 | tf_op jit(solution)/shard_map/ppermute | solution.py:42
  124.7 0.0 collective-permute-done.3
  124.7 1.7 %collective-permute-start.8 = (f32[8,128]{1,0:T(8,128)S(1)}, f32[8,128]{1,0:T(8,128)S(1)}, u32[]{:S(2)}, u32[]{:S(2)}) collective-permute-start(f32[8,128]{1,0:T(8,128)S(1)} %add_add_fusion.1), channel_id=1, source_target_pairs={{0,192},{64,128},{128,64},{192,0},{1,193},{65,129},{129,65},{193,1... | collective-permute-start | bytes 12296 | tf_op jit(solution)/shard_map/ppermute | solution.py:42
  126.4 1.2 collective-permute-start.7
  127.6 1.3 collective-permute-start.6
  128.9 0.7 collective-permute-done.8
  129.6 1.9 %collective-permute-done.7 = f32[8,128]{1,0:T(8,128)S(1)} collective-permute-done((f32[8,128]{1,0:T(8,128)S(1)}, f32[8,128]{1,0:T(8,128)S(1)}, u32[]{:S(2)}, u32[]{:S(2)}) %collective-permute-start.7) | collective-permute-done | bytes 4128 | tf_op jit(solution)/shard_map/ppermute | solution.py:42
  131.5 0.0 collective-permute-done.6
  131.5 0.0 all-gather.2.cloned.1.call-done.refs_4_
  131.5 0.0 all-to-all-done.3
  131.6 26.3 %roots.1 = (bf16[1,1024,1024]{2,1,0:T(8,128)(2,1)}, f32[32,1024]{1,0:T(8,128)}, f32[32,1024]{1,0:T(8,128)}, bf16[32,1024]{1,0:T(8,128)(2,1)}, bf16[32,1024]{1,0:T(8,128)(2,1)}) custom-call(f32[8,128]{1,0:T(8,128)S(1)} %add_add_fusion.refs_0_, s32[1,2]{1,0:T(1,128)S(1)} %copy-done.4, s32[1]{0:T(128)} %bitcast.2.refs_2_, bf16[1024,1024]{1,0:T(8,128)(2,1)S(1)} %bitcast.13, ...), custom_call_target="tpu_custom_call" | custom-call | flops 21474836480 | bytes 6291456 | tf_op jit(solution)/shard_map/roots/pallas_call | solution.py:163
  (4 shorter events, 0.1 us)
Async XLA Ops:
  7.2 6.1 %copy-start = (f32[1,32,1024]{2,1,0:T(8,128)S(1)}, f32[1,32,1024]{2,1,0:T(8,128)}, u32[]{:S(2)}) copy-start(f32[1,32,1024]{2,1,0:T(8,128)} %param.7) | copy-start | bytes 393220
  7.2 6.1 %copy-start.1 = (f32[1,32,1024]{2,1,0:T(8,128)S(1)}, f32[1,32,1024]{2,1,0:T(8,128)}, u32[]{:S(2)}) copy-start(f32[1,32,1024]{2,1,0:T(8,128)} %param.8) | copy-start | bytes 393220
  7.2 6.1 %copy-start.2 = (bf16[1,32,1024]{2,1,0:T(8,128)(2,1)S(1)}, bf16[1,32,1024]{2,1,0:T(8,128)(2,1)}, u32[]{:S(2)}) copy-start(bf16[1,32,1024]{2,1,0:T(8,128)(2,1)} %param.9) | copy-start | bytes 196612
  7.2 6.1 %copy-start.3 = (bf16[1,32,1024]{2,1,0:T(8,128)(2,1)S(1)}, bf16[1,32,1024]{2,1,0:T(8,128)(2,1)}, u32[]{:S(2)}) copy-start(bf16[1,32,1024]{2,1,0:T(8,128)(2,1)} %param.10) | copy-start | bytes 196612
  7.2 6.1 %copy-start.4 = (s32[1,2]{1,0:T(1,128)S(1)}, s32[1,2]{1,0:T(1,128)}, u32[]{:S(2)}) copy-start(s32[1,2]{1,0:T(1,128)} %refs_1_.1) | copy-start | bytes 28
  7.2 34.3 %all-to-all-start = ((bf16[8,128,1024]{2,1,0:T(8,128)(2,1)}), bf16[8,128,1024]{2,1,0:T(8,128)(2,1)}, u32[]{:S(2)}, u32[]{:S(2)}) async-start(bf16[8,128,1024]{2,1,0:T(8,128)(2,1)} %bitcast.21), calls=%async_computation | async-start | bytes 4194304 | tf_op jit(solution)/shard_map/all_to_all | solution.py:27
  13.2 118.4 %all-gather.2.cloned.1.call-start = ((), (), s32[]{:S(2)}) async-start(), calls=%async_computation.4 | async-start | bytes 4325376 | tf_op jit(solution)/shard_map/all_gather | solution.py:187
  75.9 55.7 %all-to-all-start.3 = ((bf16[8,128,1024]{2,1,0:T(8,128)(2,1)}), bf16[8,128,1024]{2,1,0:T(8,128)(2,1)S(1)}, u32[]{:S(2)}, u32[]{:S(2)}) async-start(bf16[8,128,1024]{2,1,0:T(8,128)(2,1)} %broadcast_in_dim.31), calls=%async_computation.3 | async-start | bytes 4194304 | tf_op jit(solution)/shard_map/all_to_all | solution.py:34
  82.0 35.0 %collective-permute-start.1 = (f32[8,128]{1,0:T(8,128)S(1)}, f32[8,128]{1,0:T(8,128)S(1)}, u32[]{:S(2)}, u32[]{:S(2)}) collective-permute-start(f32[8,128]{1,0:T(8,128)S(1)} %broadcast_in_dim.29), channel_id=1, source_target_pairs={{0,8},{1,9},{8,0},{9,1},{2,10},{3,11},{10,2},{11,3},{4,12},{5,13},... | collective-permute-start | bytes 12296 | tf_op jit(solution)/shard_map/ppermute | solution.py:42
  84.1 32.9 %collective-permute-start.2 = (f32[8,128]{1,0:T(8,128)S(1)}, f32[8,128]{1,0:T(8,128)S(1)}, u32[]{:S(2)}, u32[]{:S(2)}) collective-permute-start(f32[8,128]{1,0:T(8,128)S(1)} %broadcast_in_dim.29), channel_id=1, source_target_pairs={{0,9},{1,8},{8,1},{9,0},{2,11},{3,10},{10,3},{11,2},{4,13},{5,12},... | collective-permute-start | bytes 12296 | tf_op jit(solution)/shard_map/ppermute | solution.py:42
  84.1 32.9 %collective-permute-start = (f32[8,128]{1,0:T(8,128)S(1)}, f32[8,128]{1,0:T(8,128)S(1)}, u32[]{:S(2)}, u32[]{:S(2)}) collective-permute-start(f32[8,128]{1,0:T(8,128)S(1)} %broadcast_in_dim.29), channel_id=1, source_target_pairs={{0,1},{1,0},{8,9},{9,8},{2,3},{3,2},{10,11},{11,10},{4,5},{5,4},{1... | collective-permute-start | bytes 12296 | tf_op jit(solution)/shard_map/ppermute | solution.py:42
  117.7 4.2 %collective-permute-start.5 = (f32[8,128]{1,0:T(8,128)S(1)}, f32[8,128]{1,0:T(8,128)S(1)}, u32[]{:S(2)}, u32[]{:S(2)}) collective-permute-start(f32[8,128]{1,0:T(8,128)S(1)} %add_add_fusion.2), channel_id=1, source_target_pairs={{0,6},{2,4},{4,2},{6,0},{1,7},{3,5},{5,3},{7,1},{8,14},{10,12},{12... | collective-permute-start | bytes 12296 | tf_op jit(solution)/shard_map/ppermute | solution.py:42
  119.5 5.1 %collective-permute-start.4 = (f32[8,128]{1,0:T(8,128)S(1)}, f32[8,128]{1,0:T(8,128)S(1)}, u32[]{:S(2)}, u32[]{:S(2)}) collective-permute-start(f32[8,128]{1,0:T(8,128)S(1)} %add_add_fusion.2), channel_id=1, source_target_pairs={{0,4},{2,6},{4,0},{6,2},{1,5},{3,7},{5,1},{7,3},{8,12},{10,14},{12... | collective-permute-start | bytes 12296 | tf_op jit(solution)/shard_map/ppermute | solution.py:42
  120.4 4.3 %collective-permute-start.3 = (f32[8,128]{1,0:T(8,128)S(1)}, f32[8,128]{1,0:T(8,128)S(1)}, u32[]{:S(2)}, u32[]{:S(2)}) collective-permute-start(f32[8,128]{1,0:T(8,128)S(1)} %add_add_fusion.2), channel_id=1, source_target_pairs={{0,2},{2,0},{4,6},{6,4},{1,3},{3,1},{5,7},{7,5},{8,10},{10,8},{12,... | collective-permute-start | bytes 12296 | tf_op jit(solution)/shard_map/ppermute | solution.py:42
  124.7 4.9 %collective-permute-start.8 = (f32[8,128]{1,0:T(8,128)S(1)}, f32[8,128]{1,0:T(8,128)S(1)}, u32[]{:S(2)}, u32[]{:S(2)}) collective-permute-start(f32[8,128]{1,0:T(8,128)S(1)} %add_add_fusion.1), channel_id=1, source_target_pairs={{0,192},{64,128},{128,64},{192,0},{1,193},{65,129},{129,65},{193,1... | collective-permute-start | bytes 12296 | tf_op jit(solution)/shard_map/ppermute | solution.py:42
  126.4 5.1 %collective-permute-start.7 = (f32[8,128]{1,0:T(8,128)S(1)}, f32[8,128]{1,0:T(8,128)S(1)}, u32[]{:S(2)}, u32[]{:S(2)}) collective-permute-start(f32[8,128]{1,0:T(8,128)S(1)} %add_add_fusion.1), channel_id=1, source_target_pairs={{0,128},{64,192},{128,0},{192,64},{1,129},{65,193},{129,1},{193,65... | collective-permute-start | bytes 12296 | tf_op jit(solution)/shard_map/ppermute | solution.py:42
  127.6 3.9 %collective-permute-start.6 = (f32[8,128]{1,0:T(8,128)S(1)}, f32[8,128]{1,0:T(8,128)S(1)}, u32[]{:S(2)}, u32[]{:S(2)}) collective-permute-start(f32[8,128]{1,0:T(8,128)S(1)} %add_add_fusion.1), channel_id=1, source_target_pairs={{0,64},{64,0},{128,192},{192,128},{1,65},{65,1},{129,193},{193,129... | collective-permute-start | bytes 12296 | tf_op jit(solution)/shard_map/ppermute | solution.py:42
Sparse Core Ops, SparseCore 0:
  17.2 101.3 all-gather.1

commit v2 on v1

--- a/solution.py
+++ b/solution.py
@@ -35,29 +35,51 @@
     return parts.reshape(groups * value.shape[0], value.shape[1])
 
 
-def sum_of_four(value, axes):
-    others = []
-    for mask in (1, 2, 3):
-        swap = [(i, i ^ mask) for i in range(4)]
-        others.append(lax.ppermute(value, axes, swap))
-    return (value + others[0]) + (others[1] + others[2])
-
-
-def choose_kernel(due, left_stat, right_stat, left_root, right_root, chosen):
-    for k, stat, root in ((0, left_stat, left_root), (1, right_stat, right_root)):
-        chosen[k] = jnp.where(due[0, k] == 1, stat[...].astype(jnp.bfloat16), root[...])
-
-
-def choose(due, left_stat, right_stat, left_root, right_root):
-    vector = pl.BlockSpec(memory_space=pltpu.VMEM)
+def sum_over(value, axes):
+    size = lax.axis_size(axes)
+    parts = [value]
+    for mask in range(1, size):
+        swap = [(i, i ^ mask) for i in range(size)]
+        parts.append(lax.ppermute(value, axes, swap))
+    while len(parts) > 1:
+        parts = [a + b for a, b in zip(parts[::2], parts[1::2])]
+    return parts[0]
+
+
+def choose_kernel(due, left_stat, right_stat, left_root, right_root, chosen, *scratch):
+    flags, *held, sems = scratch
+    far = (due, left_stat, right_stat, left_root, right_root)
+    fetches = [
+        pltpu.make_async_copy(ref, near, sems.at[i])
+        for i, (ref, near) in enumerate(zip(far, (flags, *held)))
+    ]
+    for fetch in fetches:
+        fetch.start()
+    for fetch in fetches:
+        fetch.wait()
+    for k in range(2):
+        stat, root = held[k][...], held[2 + k][...]
+        chosen[k] = jnp.where(flags[0, k] == 1, stat.astype(jnp.bfloat16), root)
+
+
+def choose(*arrays):
+    far = pl.BlockSpec(memory_space=pltpu.HBM)
+    arrays = [pltpu.with_memory_space_constraint(a, pltpu.HBM) for a in arrays]
+    due, *rows = arrays
+    root = rows[-1]
     return pl.pallas_call(
         choose_kernel,
-        out_shape=jax.ShapeDtypeStruct((2, *left_root.shape), jnp.bfloat16),
-        in_specs=[pl.BlockSpec(memory_space=pltpu.SMEM), vector, vector, vector, vector],
-        out_specs=vector,
+        out_shape=jax.ShapeDtypeStruct((2, *root.shape), root.dtype),
+        in_specs=[far] * len(arrays),
+        out_specs=pl.BlockSpec(memory_space=pltpu.VMEM),
+        scratch_shapes=[
+            pltpu.SMEM(due.shape, due.dtype),
+            *[pltpu.VMEM(a.shape, a.dtype) for a in rows],
+            pltpu.SemaphoreType.DMA((len(arrays),)),
+        ],
         compiler_params=pltpu.CompilerParams(vmem_limit_bytes=4 * 2**20),
         name="choose",
-    )(due, left_stat, right_stat, left_root, right_root)
+    )(*arrays)
 
 
 def roots_kernel(tile, blocks, *refs):
@@ -184,15 +206,17 @@
     row_count = left_stat.shape[1]
     row_start = lax.axis_index(DP) * row_count
     chosen = choose(due, left_stat[0], right_stat[0], left_root[0], right_root[0])
+    chosen, partial = lax.optimization_barrier((chosen, grad_parts[0, 0]))
     chosen = lax.all_gather(chosen, DP, axis=1, tiled=True)
     chosen = pltpu.with_memory_space_constraint(chosen, pltpu.HBM)
 
-    rows = exchange_sum(exchange_sum(grad_parts[0, 0], WIDE), NARROW)
+    part = exchange_sum(partial, WIDE)
+    rows = exchange_sum(part, NARROW)
     chunk = spread(rows, NARROW)
     squares = jnp.sum(chunk.astype(jnp.float32) ** 2)
     total = jnp.full((8, 128), squares, jnp.float32)
-    for axes in (("zl", "c"), ("x",), ("y",)):
-        total = sum_of_four(total, axes)
+    for axes in ("c", "x", WIDE):
+        total = sum_over(total, axes)
     grad = spread(chunk, WIDE)
     place = row_start.astype(jnp.int32).reshape(1)
     update, left_new, right_new, left_out, right_out = roots(

time: 166 us -> 157 us (0.946)
  waiting for transfers between devices: 65.2 us -> 52.7 us
  starting transfers between devices: 21.4 us -> 25.8 us
    ppermute x9 -> x11, waiting for transfers between devices: 38.2 us -> 24.5 us  [sum_over(): parts.append(lax.ppermute(value, axes, swap))]
    ppermute x9 -> x11, starting transfers between devices: 10.7 us -> 15.4 us  [sum_over(): parts.append(lax.ppermute(value, axes, swap))]
  transfers between devices with their start and end apart: 12 -> 14, of which waited for: 5 -> 7; matrix products, arithmetic and copies ran while one was open for 3% -> 3% of each run, Pallas kernels for 1% -> 0%
where the time goes in v2:
time: 157 us; the launch traced here: 156 us
  waiting for transfers between devices  52.7 us (34%)
  blocking collectives  30.9 us (20%)
  Pallas kernels  28 us (18%)
  starting transfers between devices  25.8 us (16%)
  between operations  14.2 us (9%)
  other arithmetic  2.45 us (2%)
  local copies, waits for them, and re-layouts  2.26 us (1%)
    all_to_all x1, waiting for transfers between devices, exchange_sum(): parts = lax.all_to_all(parts, axes, 0, 0, tiled=True)  27.5 us
    pallas_call x1, Pallas kernels, roots(): pl.pallas_call(functools.partial(roots_kernel, tile, lax.axis_size(MP)),...  26.3 us
    ppermute x11, waiting for transfers between devices, sum_over(): parts.append(lax.ppermute(value, axes, swap))  24.5 us
    all_to_all x1, blocking collectives, exchange_sum(): parts = lax.all_to_all(parts, axes, 0, 0, tiled=True)  18.7 us
    ppermute x11, starting transfers between devices, sum_over(): parts.append(lax.ppermute(value, axes, swap))  15.4 us
    all_to_all x1, blocking collectives, spread(): parts = lax.all_to_all(copies, axes, 0, 0, tiled=True)  12.2 us
    all_to_all x1, starting transfers between devices, exchange_sum(): parts = lax.all_to_all(parts, axes, 0, 0, tiled=True)  5.84 us
    all_to_all x1, starting transfers between devices, spread(): parts = lax.all_to_all(copies, axes, 0, 0, tiled=True)  4.55 us
  transfers between devices with their start and end apart: 14, of which 7 were waited for; matrix products, arithmetic and copies ran while one was open for 3% of the time, Pallas kernels for 0%

profile of v2, /device:TPU:2, one launch (start us, length us, event | category | flops | bytes accessed | tf_op | source)
XLA Modules:
  0.0 156.3 jit_solution(12273267342751926383)
XLA Ops:
  7.2 1.7 %choose.1 = bf16[2,32,1024]{2,1,0:T(8,128)(2,1)} custom-call(s32[1,2]{1,0:T(1,128)} %refs_1_.1, f32[32,1024]{1,0:T(8,128)} %bitcast.15, f32[32,1024]{1,0:T(8,128)} %bitcast.17, bf16[32,1024]{1,0:T(8,128)(2,1)} %bitcast.22, bf16[32,1024]{1,0:T(8,128)(2,1)} %bitcast.23), custom_call_target="tpu_custom_call" | custom-call | tf_op jit(solution)/shard_map/choose/pallas_call | solution.py:70
  8.9 5.8 %all-to-all-start = ((bf16[8,128,1024]{2,1,0:T(8,128)(2,1)}), bf16[8,128,1024]{2,1,0:T(8,128)(2,1)S(1)}, u32[]{:S(2)}, u32[]{:S(2)}) async-start(bf16[8,128,1024]{2,1,0:T(8,128)(2,1)} %bitcast.20), calls=%async_computation | async-start | bytes 4194304 | tf_op jit(solution)/shard_map/all_to_all | solution.py:27
  14.7 0.0 all-gather.2.cloned.1.call-start
  14.8 0.7 all-gather.2.cloned.1.call-update
  15.5 27.5 %all-to-all-done = bf16[8,128,1024]{2,1,0:T(8,128)(2,1)S(1)} async-done(((bf16[8,128,1024]{2,1,0:T(8,128)(2,1)}), bf16[8,128,1024]{2,1,0:T(8,128)(2,1)S(1)}, u32[]{:S(2)}, u32[]{:S(2)}) %all-to-all-start) | async-done | bytes 2097184 | tf_op jit(solution)/shard_map/all_to_all | solution.py:27
  43.0 0.4 reduce_sum.33
  43.4 18.7 %all_to_all.20 = bf16[4,32,1024]{2,1,0:T(8,128)(2,1)S(1)} all-to-all(bf16[4,32,1024]{2,1,0:T(8,128)(2,1)S(1)} %bitcast.21), channel_id=1, replica_groups=mesh['y'=4,'zh'=4,'zl'=2,'x'=4,'c'=2] {'zh'}, dimensions={0} | all-to-all | bytes 524288 | tf_op jit(solution)/shard_map/all_to_all | solution.py:27
  62.2 12.2 %all_to_all.21 = bf16[4,32,1024]{2,1,0:T(8,128)(2,1)S(1)} all-to-all(bf16[4,32,1024]{2,1,0:T(8,128)(2,1)S(1)} %broadcast_in_dim.28), channel_id=1, replica_groups=mesh['y'=4,'zh'=4,'zl'=2,'x'=4,'c'=2] {'zh'}, dimensions={0} | all-to-all | bytes 524288 | tf_op jit(solution)/shard_map/all_to_all | solution.py:34
  74.3 1.6 %broadcast_in_dim.31 = bf16[8,128,1024]{2,1,0:T(8,128)(2,1)} broadcast(bf16[128,1024]{1,0:T(8,128)(2,1)S(1)} %bitcast.19), dimensions={1,2} | broadcast | bytes 2359296 | tf_op jit(solution)/shard_map/broadcast_in_dim | solution.py:33
  75.9 0.0 copy-start
  75.9 0.0 copy-start.1
  75.9 0.0 copy-start.2
  75.9 4.5 %all-to-all-start.3 = ((bf16[8,128,1024]{2,1,0:T(8,128)(2,1)}), bf16[8,128,1024]{2,1,0:T(8,128)(2,1)S(1)}, u32[]{:S(2)}, u32[]{:S(2)}) async-start(bf16[8,128,1024]{2,1,0:T(8,128)(2,1)} %broadcast_in_dim.31), calls=%async_computation.3 | async-start | bytes 4194304 | tf_op jit(solution)/shard_map/all_to_all | solution.py:34
  80.5 0.7 multiply_reduce_fusion
  81.2 0.6 broadcast_in_dim.29
  81.8 0.1 collective-permute-start
  81.9 1.2 collective-permute-done
  83.1 0.6 broadcast_add_fusion
  83.8 2.1 %collective-permute-start.2 = (f32[8,128]{1,0:T(8,128)S(1)}, f32[8,128]{1,0:T(8,128)S(1)}, u32[]{:S(2)}, u32[]{:S(2)}) collective-permute-start(f32[8,128]{1,0:T(8,128)S(1)} %broadcast_add_fusion), channel_id=1, source_target_pairs={{0,4},{2,6},{4,0},{6,2},{1,5},{3,7},{5,1},{7,3},{8,12},{10,14},{12... | collective-permute-start | bytes 12296 | tf_op jit(solution)/shard_map/ppermute | solution.py:43
  85.9 0.0 collective-permute-start.3
  85.9 2.7 %collective-permute-start.1 = (f32[8,128]{1,0:T(8,128)S(1)}, f32[8,128]{1,0:T(8,128)S(1)}, u32[]{:S(2)}, u32[]{:S(2)}) collective-permute-start(f32[8,128]{1,0:T(8,128)S(1)} %broadcast_add_fusion), channel_id=1, source_target_pairs={{0,2},{2,0},{4,6},{6,4},{1,3},{3,1},{5,7},{7,5},{8,10},{10,8},{12,... | collective-permute-start | bytes 12296 | tf_op jit(solution)/shard_map/ppermute | solution.py:43
  88.5 0.4 collective-permute-done.2
  89.0 0.5 collective-permute-done.3
  89.5 0.6 collective-permute-done.1
  90.1 0.7 add_add_fusion.1
  90.8 4.2 %collective-permute-start.10 = (f32[8,128]{1,0:T(8,128)S(1)}, f32[8,128]{1,0:T(8,128)S(1)}, u32[]{:S(2)}, u32[]{:S(2)}) collective-permute-start(f32[8,128]{1,0:T(8,128)S(1)} %add_add_fusion.1), channel_id=1, source_target_pairs={{0,200},{8,192},{64,136},{72,128},{128,72},{136,64},{192,8},{200,0... | collective-permute-start | bytes 12296 | tf_op jit(solution)/shard_map/ppermute | solution.py:43
  95.0 0.6 collective-permute-start.9
  95.6 1.8 %collective-permute-start.8 = (f32[8,128]{1,0:T(8,128)S(1)}, f32[8,128]{1,0:T(8,128)S(1)}, u32[]{:S(2)}, u32[]{:S(2)}) collective-permute-start(f32[8,128]{1,0:T(8,128)S(1)} %add_add_fusion.1), channel_id=1, source_target_pairs={{0,136},{8,128},{64,200},{72,192},{128,8},{136,0},{192,72},{200,64... | collective-permute-start | bytes 12296 | tf_op jit(solution)/shard_map/ppermute | solution.py:43
  97.3 1.3 collective-permute-start.7
  98.6 1.6 %collective-permute-start.6 = (f32[8,128]{1,0:T(8,128)S(1)}, f32[8,128]{1,0:T(8,128)S(1)}, u32[]{:S(2)}, u32[]{:S(2)}) collective-permute-start(f32[8,128]{1,0:T(8,128)S(1)} %add_add_fusion.1), channel_id=1, source_target_pairs={{0,72},{8,64},{64,8},{72,0},{128,200},{136,192},{192,136},{200,128... | collective-permute-start | bytes 12296 | tf_op jit(solution)/shard_map/ppermute | solution.py:43
  100.2 19.2 %collective-permute-done.10 = f32[8,128]{1,0:T(8,128)S(1)} collective-permute-done((f32[8,128]{1,0:T(8,128)S(1)}, f32[8,128]{1,0:T(8,128)S(1)}, u32[]{:S(2)}, u32[]{:S(2)}) %collective-permute-start.10) | collective-permute-done | bytes 4128 | tf_op jit(solution)/shard_map/ppermute | solution.py:43
  119.4 0.0 collective-permute-start.5
  119.4 0.0 collective-permute-done.9
  119.4 1.1 collective-permute-start.4
  120.5 0.0 collective-permute-done.8
  120.5 0.0 collective-permute-done.7
  120.5 0.0 collective-permute-done.6
  120.5 2.5 %collective-permute-done.5 = f32[8,128]{1,0:T(8,128)S(1)} collective-permute-done((f32[8,128]{1,0:T(8,128)S(1)}, f32[8,128]{1,0:T(8,128)S(1)}, u32[]{:S(2)}, u32[]{:S(2)}) %collective-permute-start.5) | collective-permute-done | bytes 4128 | tf_op jit(solution)/shard_map/ppermute | solution.py:43
  123.0 0.0 collective-permute-done.4
  123.1 0.0 all-gather.2.cloned.1.call-done.refs_4_
  123.1 0.0 all-to-all-done.3
  123.1 0.0 copy-done
  123.1 0.0 copy-done.1
  123.1 0.0 copy-done.2
  123.1 26.3 %roots.1 = (bf16[1,1024,1024]{2,1,0:T(8,128)(2,1)}, f32[32,1024]{1,0:T(8,128)}, f32[32,1024]{1,0:T(8,128)}, bf16[32,1024]{1,0:T(8,128)(2,1)}, bf16[32,1024]{1,0:T(8,128)(2,1)}) custom-call(f32[8,128]{1,0:T(8,128)S(1)} %add_add_fusion.refs_0_, s32[1,2]{1,0:T(1,128)S(1)} %copy-done.2, s32[1]{0:T(128)} %bitcast.7.refs_2_, bf16[1024,1024]{1,0:T(8,128)(2,1)S(1)} %bitcast.14, ...), custom_call_target="tpu_custom_call" | custom-call | flops 21474836480 | bytes 6291456 | tf_op jit(solution)/shard_map/roots/pallas_call | solution.py:185
  (3 shorter events, 0.1 us)
Async XLA Ops:
  8.9 34.1 %all-to-all-start = ((bf16[8,128,1024]{2,1,0:T(8,128)(2,1)}), bf16[8,128,1024]{2,1,0:T(8,128)(2,1)S(1)}, u32[]{:S(2)}, u32[]{:S(2)}) async-start(bf16[8,128,1024]{2,1,0:T(8,128)(2,1)} %bitcast.20), calls=%async_computation | async-start | bytes 4194304 | tf_op jit(solution)/shard_map/all_to_all | solution.py:27
  14.7 108.4 %all-gather.2.cloned.1.call-start = ((), (), s32[]{:S(2)}) async-start(), calls=%async_computation.4 | async-start | bytes 4325376 | tf_op jit(solution)/shard_map/all_gather | solution.py:210
  75.9 47.2 %copy-start = (f32[1,32,1024]{2,1,0:T(8,128)S(1)}, f32[1,32,1024]{2,1,0:T(8,128)}, u32[]{:S(2)}) copy-start(f32[1,32,1024]{2,1,0:T(8,128)} %param.7) | copy-start | bytes 393220
  75.9 47.2 %copy-start.1 = (f32[1,32,1024]{2,1,0:T(8,128)S(1)}, f32[1,32,1024]{2,1,0:T(8,128)}, u32[]{:S(2)}) copy-start(f32[1,32,1024]{2,1,0:T(8,128)} %param.8) | copy-start | bytes 393220
  75.9 47.2 %copy-start.2 = (s32[1,2]{1,0:T(1,128)S(1)}, s32[1,2]{1,0:T(1,128)}, u32[]{:S(2)}) copy-start(s32[1,2]{1,0:T(1,128)} %refs_1_.1) | copy-start | bytes 28
  75.9 47.2 %all-to-all-start.3 = ((bf16[8,128,1024]{2,1,0:T(8,128)(2,1)}), bf16[8,128,1024]{2,1,0:T(8,128)(2,1)S(1)}, u32[]{:S(2)}, u32[]{:S(2)}) async-start(bf16[8,128,1024]{2,1,0:T(8,128)(2,1)} %broadcast_in_dim.31), calls=%async_computation.3 | async-start | bytes 4194304 | tf_op jit(solution)/shard_map/all_to_all | solution.py:34
  81.8 1.3 collective-permute-start
  83.8 5.2 %collective-permute-start.2 = (f32[8,128]{1,0:T(8,128)S(1)}, f32[8,128]{1,0:T(8,128)S(1)}, u32[]{:S(2)}, u32[]{:S(2)}) collective-permute-start(f32[8,128]{1,0:T(8,128)S(1)} %broadcast_add_fusion), channel_id=1, source_target_pairs={{0,4},{2,6},{4,0},{6,2},{1,5},{3,7},{5,1},{7,3},{8,12},{10,14},{12... | collective-permute-start | bytes 12296 | tf_op jit(solution)/shard_map/ppermute | solution.py:43
  85.9 3.6 %collective-permute-start.3 = (f32[8,128]{1,0:T(8,128)S(1)}, f32[8,128]{1,0:T(8,128)S(1)}, u32[]{:S(2)}, u32[]{:S(2)}) collective-permute-start(f32[8,128]{1,0:T(8,128)S(1)} %broadcast_add_fusion), channel_id=1, source_target_pairs={{0,6},{2,4},{4,2},{6,0},{1,7},{3,5},{5,3},{7,1},{8,14},{10,12},{12... | collective-permute-start | bytes 12296 | tf_op jit(solution)/shard_map/ppermute | solution.py:43
  85.9 4.3 %collective-permute-start.1 = (f32[8,128]{1,0:T(8,128)S(1)}, f32[8,128]{1,0:T(8,128)S(1)}, u32[]{:S(2)}, u32[]{:S(2)}) collective-permute-start(f32[8,128]{1,0:T(8,128)S(1)} %broadcast_add_fusion), channel_id=1, source_target_pairs={{0,2},{2,0},{4,6},{6,4},{1,3},{3,1},{5,7},{7,5},{8,10},{10,8},{12,... | collective-permute-start | bytes 12296 | tf_op jit(solution)/shard_map/ppermute | solution.py:43
  90.8 28.7 %collective-permute-start.10 = (f32[8,128]{1,0:T(8,128)S(1)}, f32[8,128]{1,0:T(8,128)S(1)}, u32[]{:S(2)}, u32[]{:S(2)}) collective-permute-start(f32[8,128]{1,0:T(8,128)S(1)} %add_add_fusion.1), channel_id=1, source_target_pairs={{0,200},{8,192},{64,136},{72,128},{128,72},{136,64},{192,8},{200,0... | collective-permute-start | bytes 12296 | tf_op jit(solution)/shard_map/ppermute | solution.py:43
  95.0 24.4 %collective-permute-start.9 = (f32[8,128]{1,0:T(8,128)S(1)}, f32[8,128]{1,0:T(8,128)S(1)}, u32[]{:S(2)}, u32[]{:S(2)}) collective-permute-start(f32[8,128]{1,0:T(8,128)S(1)} %add_add_fusion.1), channel_id=1, source_target_pairs={{0,192},{8,200},{64,128},{72,136},{128,64},{136,72},{192,0},{200,8... | collective-permute-start | bytes 12296 | tf_op jit(solution)/shard_map/ppermute | solution.py:43
  95.6 24.9 %collective-permute-start.8 = (f32[8,128]{1,0:T(8,128)S(1)}, f32[8,128]{1,0:T(8,128)S(1)}, u32[]{:S(2)}, u32[]{:S(2)}) collective-permute-start(f32[8,128]{1,0:T(8,128)S(1)} %add_add_fusion.1), channel_id=1, source_target_pairs={{0,136},{8,128},{64,200},{72,192},{128,8},{136,0},{192,72},{200,64... | collective-permute-start | bytes 12296 | tf_op jit(solution)/shard_map/ppermute | solution.py:43
  97.3 23.2 %collective-permute-start.7 = (f32[8,128]{1,0:T(8,128)S(1)}, f32[8,128]{1,0:T(8,128)S(1)}, u32[]{:S(2)}, u32[]{:S(2)}) collective-permute-start(f32[8,128]{1,0:T(8,128)S(1)} %add_add_fusion.1), channel_id=1, source_target_pairs={{0,128},{8,136},{64,192},{72,200},{128,0},{136,8},{192,64},{200,72... | collective-permute-start | bytes 12296 | tf_op jit(solution)/shard_map/ppermute | solution.py:43
  98.6 21.9 %collective-permute-start.6 = (f32[8,128]{1,0:T(8,128)S(1)}, f32[8,128]{1,0:T(8,128)S(1)}, u32[]{:S(2)}, u32[]{:S(2)}) collective-permute-start(f32[8,128]{1,0:T(8,128)S(1)} %add_add_fusion.1), channel_id=1, source_target_pairs={{0,72},{8,64},{64,8},{72,0},{128,200},{136,192},{192,136},{200,128... | collective-permute-start | bytes 12296 | tf_op jit(solution)/shard_map/ppermute | solution.py:43
  119.4 3.6 %collective-permute-start.5 = (f32[8,128]{1,0:T(8,128)S(1)}, f32[8,128]{1,0:T(8,128)S(1)}, u32[]{:S(2)}, u32[]{:S(2)}) collective-permute-start(f32[8,128]{1,0:T(8,128)S(1)} %add_add_fusion.1), channel_id=1, source_target_pairs={{0,64},{8,72},{64,0},{72,8},{128,192},{136,200},{192,128},{200,136... | collective-permute-start | bytes 12296 | tf_op jit(solution)/shard_map/ppermute | solution.py:43
  119.4 3.6 %collective-permute-start.4 = (f32[8,128]{1,0:T(8,128)S(1)}, f32[8,128]{1,0:T(8,128)S(1)}, u32[]{:S(2)}, u32[]{:S(2)}) collective-permute-start(f32[8,128]{1,0:T(8,128)S(1)} %add_add_fusion.1), channel_id=1, source_target_pairs={{0,8},{8,0},{64,72},{72,64},{128,136},{136,128},{192,200},{200,192... | collective-permute-start | bytes 12296 | tf_op jit(solution)/shard_map/ppermute | solution.py:43
Sparse Core Ops, SparseCore 0:
  18.7 101.7 all-gather.1

commit v3 on v2

--- a/solution.py
+++ b/solution.py
@@ -85,11 +85,23 @@
 def roots_kernel(tile, blocks, *refs):
     total, due, place, grad, chosen, left_stat, right_stat = refs[:7]
     update, left_new, right_new, left_out, right_out = refs[7:12]
-    picked, flipped, first, second, mixed, used, x, fourth, block, sems, sent = refs[12:]
+    picked, flipped, first, second, mixed, used, x, fourth, block = refs[12:21]
+    new_rows, out_rows, sems, sent = refs[21:]
+    sends = []
+
+    def send(source, target):
+        sends.append(pltpu.make_async_copy(source, target, sent.at[len(sends)]))
+        sends[-1].start()
+
     order = grad.shape[0]
     rows = left_stat.shape[0]
     weight = (1.0 - decay) / order
     columns = [slice(n * tile, (n + 1) * tile) for n in range(order // tile)]
+    step = 256
+    corners = [
+        (slice(i, order), slice(i, i + step), slice(i + step, order))
+        for i in range(0, order, step)
+    ]
     fetches = [
         pltpu.make_async_copy(chosen.at[k], picked.at[k], sems.at[k]) for k in range(2)
     ]
@@ -139,38 +151,50 @@
             first[:, cols] = (jnp.where(row == col, 1.25, 0.0) - statistic * shrink).astype(
                 jnp.bfloat16
             )
-        new[...] = stat[...] * decay + block[mine, :] * weight
-        for cols in columns:
-            square = dot(first[...], first[:, cols], across).astype(jnp.bfloat16)
-            second[:, cols] = square
-            mixed[:, cols] = (
-                5.0 * first[:, cols].astype(jnp.float32) - 4.0 * square.astype(jnp.float32)
-            ).astype(jnp.bfloat16)
-            if k == 0:
+        new_rows[k] = stat[...] * decay + block[mine, :] * weight
+        send(new_rows.at[k], new)
+        if k == 0:
+            for cols in columns:
                 flipped[cols, :] = grad[:, cols].T
-        for cols in columns:
-            fourth[:, cols] = dot(second[...], second[:, cols], across).astype(jnp.bfloat16)
-        for cols in columns:
-            inner = dot(fourth[...], mixed[:, cols], across)
-            root = lift * (5.0 * first[:, cols].astype(jnp.float32) - inner)
-            used[:, cols] = jnp.where(
-                due[0, k] == 1, root.astype(jnp.bfloat16), picked[k, :, cols]
-            )
-        out[...] = used[mine, :]
+        for rest, cols, beyond in corners:
+            square = dot(first[rest, :], first[:, cols], across).astype(jnp.bfloat16)
+            second[rest, cols] = square
+            parts = [(rest, cols)]
+            if beyond.start < order:
+                second[cols, beyond] = square[step:].T
+                parts.append((cols, beyond))
+            for here, there in parts:
+                mixed[here, there] = (
+                    5.0 * first[here, there].astype(jnp.float32)
+                    - 4.0 * second[here, there].astype(jnp.float32)
+                ).astype(jnp.bfloat16)
+        for rest, cols, beyond in corners:
+            power = dot(second[rest, :], second[:, cols], across).astype(jnp.bfloat16)
+            fourth[rest, cols] = power
+            if beyond.start < order:
+                fourth[cols, beyond] = power[step:].T
+        for rest, cols, beyond in corners:
+            inner = dot(fourth[rest, :], mixed[:, cols], across)
+            root = lift[:, :step] * (5.0 * first[rest, cols].astype(jnp.float32) - inner)
+            root = root.astype(jnp.bfloat16)
+            used[rest, cols] = jnp.where(due[0, k] == 1, root, picked[k, rest, cols])
+            if beyond.start < order:
+                flip = root[step:].T
+                used[cols, beyond] = jnp.where(due[0, k] == 1, flip, picked[k, cols, beyond])
+        out_rows[k] = used[mine, :]
+        send(out_rows.at[k], out)
 
     root_of(0, left_stat, left_new, left_out)
     for cols in columns:
         x[:, cols] = dot(used[...], grad[:, cols], across).astype(jnp.bfloat16)
     root_of(1, right_stat, right_new, right_out)
-    sends = []
-    for n, cols in enumerate(columns):
-        fourth[:, cols] = (dot(x[...], used[:, cols], across) * factor).astype(jnp.bfloat16)
-        sends.append(
-            pltpu.make_async_copy(fourth.at[:, cols], update.at[0, :, cols], sent.at[n])
-        )
-        sends[-1].start()
-    for send in sends:
-        send.wait()
+    for start in range(0, order, 256):
+        cols = slice(start, start + 256)
+        scaled = dot(x[...], used[:, cols], across) * factor[:, :256]
+        fourth[:, cols] = scaled.astype(jnp.bfloat16)
+        send(fourth.at[:, cols], update.at[0, :, cols])
+    for copy in sends:
+        copy.wait()
 
 
 def roots(total, due, place, grad, chosen, left_stat, right_stat):
@@ -186,13 +210,15 @@
         functools.partial(roots_kernel, tile, lax.axis_size(MP)),
         out_shape=(jax.ShapeDtypeStruct((1, order, order), jnp.bfloat16), new, new, out, out),
         in_specs=[vector, scalar, scalar, vector, far, vector, vector],
-        out_specs=(far, vector, vector, vector, vector),
+        out_specs=(far,) * 5,
         scratch_shapes=[
             pltpu.VMEM((2, order, order), jnp.bfloat16),
             *([square] * 7),
             pltpu.VMEM((order, order), jnp.float32),
+            pltpu.VMEM((2, *left_stat.shape), jnp.float32),
+            pltpu.VMEM((2, *left_stat.shape), jnp.bfloat16),
             pltpu.SemaphoreType.DMA((2,)),
-            pltpu.SemaphoreType.DMA((order // tile,)),
+            pltpu.SemaphoreType.DMA((4 + order // 256,)),
         ],
         cost_estimate=pl.CostEstimate(
             flops=10 * 2 * order**3, transcendentals=0, bytes_accessed=6 * 2**20
@@ -212,12 +238,12 @@
 
     part = exchange_sum(partial, WIDE)
     rows = exchange_sum(part, NARROW)
-    chunk = spread(rows, NARROW)
+    chunk = spread(rows, ("zl", "zh"))
     squares = jnp.sum(chunk.astype(jnp.float32) ** 2)
     total = jnp.full((8, 128), squares, jnp.float32)
-    for axes in ("c", "x", WIDE):
+    for axes in ("c", "x", "y"):
         total = sum_over(total, axes)
-    grad = spread(chunk, WIDE)
+    grad = spread(chunk, "y")
     place = row_start.astype(jnp.int32).reshape(1)
     update, left_new, right_new, left_out, right_out = roots(
         total, due, place, grad, chosen, left_stat[0], right_stat[0]

time: 157 us -> 143 us (0.911)
  blocking collectives: 30.9 us -> 74.3 us
  waiting for transfers between devices: 52.7 us -> 13.5 us
  starting transfers between devices: 25.8 us -> 12.9 us
  Pallas kernels: 28 us -> 22.5 us
    all_to_all x1 -> x2, blocking collectives: 18.7 us -> 54.1 us  [exchange_sum(): parts = lax.all_to_all(parts, axes, 0, 0, tiled=True)]
    all_to_all x1 -> x0, waiting for transfers between devices: 27.5 us -> none  [exchange_sum(): parts = lax.all_to_all(parts, axes, 0, 0, tiled=True)]
    ppermute x11 -> x7, waiting for transfers between devices: 24.5 us -> 13.4 us  [sum_over(): parts.append(lax.ppermute(value, axes, swap))]
    all_to_all x1, blocking collectives: 12.2 us -> 20.2 us  [spread(): parts = lax.all_to_all(copies, axes, 0, 0, tiled=True)]
    ppermute x11 -> x7, starting transfers between devices: 15.4 us -> 9.12 us  [sum_over(): parts.append(lax.ppermute(value, axes, swap))]
    all_to_all x1 -> x0, starting transfers between devices: 5.84 us -> none  [exchange_sum(): parts = lax.all_to_all(parts, axes, 0, 0, tiled=True)]
    pallas_call x1, Pallas kernels: 26.3 us -> 20.8 us  [roots(): pl.pallas_call(functools.partial(roots_kernel, tile, lax.axis_size(MP)),...]
  transfers between devices with their start and end apart: 14 -> 9, of which waited for: 7 -> 5; matrix products, arithmetic and copies ran while one was open for 3% -> 3% of each run, Pallas kernels for 0% -> 0%
where the time goes in v3:
time: 143 us; the launch traced here: 142 us
  blocking collectives  74.3 us (52%)
  Pallas kernels  22.5 us (16%)
  between operations  14.2 us (10%)
  waiting for transfers between devices  13.5 us (9%)
  starting transfers between devices  12.9 us (9%)
  other arithmetic  2.58 us (2%)
  local copies, waits for them, and re-layouts  2.3 us (2%)
    all_to_all x2, blocking collectives, exchange_sum(): parts = lax.all_to_all(parts, axes, 0, 0, tiled=True)  54.1 us
    pallas_call x1, Pallas kernels, roots(): pl.pallas_call(functools.partial(roots_kernel, tile, lax.axis_size(MP)),...  20.8 us
    all_to_all x1, blocking collectives, spread(): parts = lax.all_to_all(copies, axes, 0, 0, tiled=True)  20.2 us
    ppermute x7, waiting for transfers between devices, sum_over(): parts.append(lax.ppermute(value, axes, swap))  13.4 us
    ppermute x7, starting transfers between devices, sum_over(): parts.append(lax.ppermute(value, axes, swap))  9.12 us
    all_to_all x1, starting transfers between devices, spread(): parts = lax.all_to_all(copies, axes, 0, 0, tiled=True)  3.74 us
  transfers between devices with their start and end apart: 9, of which 5 were waited for; matrix products, arithmetic and copies ran while one was open for 3% of the time, Pallas kernels for 0%

profile of v3, /device:TPU:2, one launch (start us, length us, event | category | flops | bytes accessed | tf_op | source)
XLA Modules:
  0.0 142.2 jit_solution(3008794860823344859)
XLA Ops:
  7.2 0.0 all-gather.2.cloned.1.call-start
  7.2 1.7 %choose.1 = bf16[2,32,1024]{2,1,0:T(8,128)(2,1)} custom-call(s32[1,2]{1,0:T(1,128)} %refs_1_.1, f32[32,1024]{1,0:T(8,128)} %bitcast.15, f32[32,1024]{1,0:T(8,128)} %bitcast.17, bf16[32,1024]{1,0:T(8,128)(2,1)} %bitcast.22, bf16[32,1024]{1,0:T(8,128)(2,1)} %bitcast.23), custom_call_target="tpu_custom_call" | custom-call | tf_op jit(solution)/shard_map/choose/pallas_call | solution.py:70
  8.9 0.0 all-gather.2.cloned.1.call-update
  9.0 35.7 %all_to_all.20 = bf16[8,128,1024]{2,1,0:T(8,128)(2,1)S(1)} all-to-all(bf16[8,128,1024]{2,1,0:T(8,128)(2,1)} %bitcast.20), channel_id=1, replica_groups=mesh['y'=4,'zh'=4,'zl'=2,'x'=4,'c'=2] {'y','zl'}, dimensions={0} | all-to-all | bytes 4194304 | tf_op jit(solution)/shard_map/all_to_all | solution.py:27
  44.7 0.4 reduce_sum.33
  45.0 18.4 %all_to_all.21 = bf16[4,32,1024]{2,1,0:T(8,128)(2,1)S(1)} all-to-all(bf16[4,32,1024]{2,1,0:T(8,128)(2,1)S(1)} %bitcast.21), channel_id=1, replica_groups=mesh['y'=4,'zh'=4,'zl'=2,'x'=4,'c'=2] {'zh'}, dimensions={0} | all-to-all | bytes 524288 | tf_op jit(solution)/shard_map/all_to_all | solution.py:27
  63.4 0.1 broadcast_in_dim.28
  63.5 20.2 %all_to_all.22 = bf16[8,32,1024]{2,1,0:T(8,128)(2,1)S(1)} all-to-all(bf16[8,32,1024]{2,1,0:T(8,128)(2,1)S(1)} %broadcast_in_dim.28), channel_id=1, replica_groups=mesh['y'=4,'zh'=4,'zl'=2,'x'=4,'c'=2] {'zl','zh'}, dimensions={0} | all-to-all | bytes 1048576 | tf_op jit(solution)/shard_map/all_to_all | solution.py:34
  83.7 1.6 %broadcast_in_dim.31 = bf16[4,256,1024]{2,1,0:T(8,128)(2,1)} broadcast(bf16[256,1024]{1,0:T(8,128)(2,1)S(1)} %bitcast.19), dimensions={1,2} | broadcast | bytes 2621440 | tf_op jit(solution)/shard_map/broadcast_in_dim | solution.py:33
  85.3 0.0 copy-start
  85.3 0.0 copy-start.1
  85.3 0.0 copy-start.2
  85.3 3.7 %all-to-all-start.3 = ((bf16[4,256,1024]{2,1,0:T(8,128)(2,1)}), bf16[4,256,1024]{2,1,0:T(8,128)(2,1)S(1)}, u32[]{:S(2)}, u32[]{:S(2)}) async-start(bf16[4,256,1024]{2,1,0:T(8,128)(2,1)} %broadcast_in_dim.31), calls=%async_computation.3 | async-start | bytes 4194304 | tf_op jit(solution)/shard_map/all_to_all | solution.py:34
  89.1 0.9 multiply_reduce_fusion
  89.9 0.6 broadcast_in_dim.29
  90.6 0.1 collective-permute-start
  90.7 1.2 collective-permute-done
  91.9 0.6 broadcast_add_fusion
  92.5 2.3 %collective-permute-start.2 = (f32[8,128]{1,0:T(8,128)S(1)}, f32[8,128]{1,0:T(8,128)S(1)}, u32[]{:S(2)}, u32[]{:S(2)}) collective-permute-start(f32[8,128]{1,0:T(8,128)S(1)} %broadcast_add_fusion), channel_id=1, source_target_pairs={{0,4},{2,6},{4,0},{6,2},{1,5},{3,7},{5,1},{7,3},{8,12},{10,14},{12... | collective-permute-start | bytes 12296 | tf_op jit(solution)/shard_map/ppermute | solution.py:43
  94.8 0.0 collective-permute-start.3
  94.8 2.5 %collective-permute-start.1 = (f32[8,128]{1,0:T(8,128)S(1)}, f32[8,128]{1,0:T(8,128)S(1)}, u32[]{:S(2)}, u32[]{:S(2)}) collective-permute-start(f32[8,128]{1,0:T(8,128)S(1)} %broadcast_add_fusion), channel_id=1, source_target_pairs={{0,2},{2,0},{4,6},{6,4},{1,3},{3,1},{5,7},{7,5},{8,10},{10,8},{12,... | collective-permute-start | bytes 12296 | tf_op jit(solution)/shard_map/ppermute | solution.py:43
  97.3 0.4 collective-permute-done.2
  97.7 0.7 collective-permute-done.3
  98.4 0.5 collective-permute-done.1
  98.9 0.7 add_add_fusion.1
  99.5 3.3 %collective-permute-start.6 = (f32[8,128]{1,0:T(8,128)S(1)}, f32[8,128]{1,0:T(8,128)S(1)}, u32[]{:S(2)}, u32[]{:S(2)}) collective-permute-start(f32[8,128]{1,0:T(8,128)S(1)} %add_add_fusion.1), channel_id=1, source_target_pairs={{0,192},{64,128},{128,64},{192,0},{1,193},{65,129},{129,65},{193,1... | collective-permute-start | bytes 12296 | tf_op jit(solution)/shard_map/ppermute | solution.py:43
  102.8 0.9 collective-permute-start.5
  103.7 0.1 collective-permute-start.4
  103.8 10.7 %collective-permute-done.6 = f32[8,128]{1,0:T(8,128)S(1)} collective-permute-done((f32[8,128]{1,0:T(8,128)S(1)}, f32[8,128]{1,0:T(8,128)S(1)}, u32[]{:S(2)}, u32[]{:S(2)}) %collective-permute-start.6) | collective-permute-done | bytes 4128 | tf_op jit(solution)/shard_map/ppermute | solution.py:43
  114.5 0.0 collective-permute-done.5
  114.5 0.0 collective-permute-done.4
  114.5 0.0 all-to-all-done.3
  114.5 0.0 all-gather.2.cloned.1.call-done.refs_4_
  114.5 0.0 copy-done
  114.6 0.0 copy-done.1
  114.6 0.0 copy-done.2
  114.6 20.8 %roots.1 = (bf16[1,1024,1024]{2,1,0:T(8,128)(2,1)}, f32[32,1024]{1,0:T(8,128)}, f32[32,1024]{1,0:T(8,128)}, bf16[32,1024]{1,0:T(8,128)(2,1)}, bf16[32,1024]{1,0:T(8,128)(2,1)}) custom-call(f32[8,128]{1,0:T(8,128)S(1)} %add_add_fusion.refs_0_, s32[1,2]{1,0:T(1,128)S(1)} %copy-done.2, s32[1]{0:T(128)} %bitcast.7.refs_2_, bf16[1024,1024]{1,0:T(8,128)(2,1)S(1)} %bitcast.14, ...), custom_call_target="tpu_custom_call" | custom-call | flops 21474836480 | bytes 6291456 | tf_op jit(solution)/shard_map/roots/pallas_call | solution.py:209
  (2 shorter events, 0.0 us)
Async XLA Ops:
  7.2 107.4 %all-gather.2.cloned.1.call-start = ((), (), s32[]{:S(2)}) async-start(), calls=%async_computation.4 | async-start | bytes 4325376 | tf_op jit(solution)/shard_map/all_gather | solution.py:236
  85.3 29.2 %copy-start = (f32[1,32,1024]{2,1,0:T(8,128)S(1)}, f32[1,32,1024]{2,1,0:T(8,128)}, u32[]{:S(2)}) copy-start(f32[1,32,1024]{2,1,0:T(8,128)} %param.7) | copy-start | bytes 393220
  85.3 29.2 %copy-start.1 = (f32[1,32,1024]{2,1,0:T(8,128)S(1)}, f32[1,32,1024]{2,1,0:T(8,128)}, u32[]{:S(2)}) copy-start(f32[1,32,1024]{2,1,0:T(8,128)} %param.8) | copy-start | bytes 393220
  85.3 29.2 %copy-start.2 = (s32[1,2]{1,0:T(1,128)S(1)}, s32[1,2]{1,0:T(1,128)}, u32[]{:S(2)}) copy-start(s32[1,2]{1,0:T(1,128)} %refs_1_.1) | copy-start | bytes 28
  85.3 29.2 %all-to-all-start.3 = ((bf16[4,256,1024]{2,1,0:T(8,128)(2,1)}), bf16[4,256,1024]{2,1,0:T(8,128)(2,1)S(1)}, u32[]{:S(2)}, u32[]{:S(2)}) async-start(bf16[4,256,1024]{2,1,0:T(8,128)(2,1)} %broadcast_in_dim.31), calls=%async_computation.3 | async-start | bytes 4194304 | tf_op jit(solution)/shard_map/all_to_all | solution.py:34
  90.6 1.3 collective-permute-start
  92.5 5.2 %collective-permute-start.2 = (f32[8,128]{1,0:T(8,128)S(1)}, f32[8,128]{1,0:T(8,128)S(1)}, u32[]{:S(2)}, u32[]{:S(2)}) collective-permute-start(f32[8,128]{1,0:T(8,128)S(1)} %broadcast_add_fusion), channel_id=1, source_target_pairs={{0,4},{2,6},{4,0},{6,2},{1,5},{3,7},{5,1},{7,3},{8,12},{10,14},{12... | collective-permute-start | bytes 12296 | tf_op jit(solution)/shard_map/ppermute | solution.py:43
  94.8 3.6 %collective-permute-start.3 = (f32[8,128]{1,0:T(8,128)S(1)}, f32[8,128]{1,0:T(8,128)S(1)}, u32[]{:S(2)}, u32[]{:S(2)}) collective-permute-start(f32[8,128]{1,0:T(8,128)S(1)} %broadcast_add_fusion), channel_id=1, source_target_pairs={{0,6},{2,4},{4,2},{6,0},{1,7},{3,5},{5,3},{7,1},{8,14},{10,12},{12... | collective-permute-start | bytes 12296 | tf_op jit(solution)/shard_map/ppermute | solution.py:43
  94.8 4.1 %collective-permute-start.1 = (f32[8,128]{1,0:T(8,128)S(1)}, f32[8,128]{1,0:T(8,128)S(1)}, u32[]{:S(2)}, u32[]{:S(2)}) collective-permute-start(f32[8,128]{1,0:T(8,128)S(1)} %broadcast_add_fusion), channel_id=1, source_target_pairs={{0,2},{2,0},{4,6},{6,4},{1,3},{3,1},{5,7},{7,5},{8,10},{10,8},{12,... | collective-permute-start | bytes 12296 | tf_op jit(solution)/shard_map/ppermute | solution.py:43
  99.5 14.9 %collective-permute-start.6 = (f32[8,128]{1,0:T(8,128)S(1)}, f32[8,128]{1,0:T(8,128)S(1)}, u32[]{:S(2)}, u32[]{:S(2)}) collective-permute-start(f32[8,128]{1,0:T(8,128)S(1)} %add_add_fusion.1), channel_id=1, source_target_pairs={{0,192},{64,128},{128,64},{192,0},{1,193},{65,129},{129,65},{193,1... | collective-permute-start | bytes 12296 | tf_op jit(solution)/shard_map/ppermute | solution.py:43
  102.8 11.7 %collective-permute-start.5 = (f32[8,128]{1,0:T(8,128)S(1)}, f32[8,128]{1,0:T(8,128)S(1)}, u32[]{:S(2)}, u32[]{:S(2)}) collective-permute-start(f32[8,128]{1,0:T(8,128)S(1)} %add_add_fusion.1), channel_id=1, source_target_pairs={{0,128},{64,192},{128,0},{192,64},{1,129},{65,193},{129,1},{193,65... | collective-permute-start | bytes 12296 | tf_op jit(solution)/shard_map/ppermute | solution.py:43
  103.7 10.8 %collective-permute-start.4 = (f32[8,128]{1,0:T(8,128)S(1)}, f32[8,128]{1,0:T(8,128)S(1)}, u32[]{:S(2)}, u32[]{:S(2)}) collective-permute-start(f32[8,128]{1,0:T(8,128)S(1)} %add_add_fusion.1), channel_id=1, source_target_pairs={{0,64},{64,0},{128,192},{192,128},{1,65},{65,1},{129,193},{193,129... | collective-permute-start | bytes 12296 | tf_op jit(solution)/shard_map/ppermute | solution.py:43
Sparse Core Ops, SparseCore 0:
  11.1 90.7 all-gather.1

commit v4 on v3

--- a/solution.py
+++ b/solution.py
@@ -44,6 +44,11 @@
     while len(parts) > 1:
         parts = [a + b for a, b in zip(parts[::2], parts[1::2])]
     return parts[0]
+
+
+def partner(value, axis, mask):
+    swap = [(i, i ^ mask) for i in range(lax.axis_size(axis))]
+    return lax.ppermute(value, axis, swap)
 
 
 def choose_kernel(due, left_stat, right_stat, left_root, right_root, chosen, *scratch):
@@ -83,17 +88,18 @@
 
 
 def roots_kernel(tile, blocks, *refs):
-    total, due, place, grad, chosen, left_stat, right_stat = refs[:7]
-    update, left_new, right_new, left_out, right_out = refs[7:12]
-    picked, flipped, first, second, mixed, used, x, fourth, block = refs[12:21]
-    new_rows, out_rows, sems, sent = refs[21:]
+    total, due, place = refs[:3]
+    chunk, next_one, last_one, far_half, far_other, chosen, left_stat, right_stat = refs[3:11]
+    update, left_new, right_new, left_out, right_out = refs[11:16]
+    picked, grad, flipped, first, second, mixed, used, x, fourth, block = refs[16:26]
+    new_rows, out_rows, sems, sent = refs[26:]
     sends = []
 
     def send(source, target):
         sends.append(pltpu.make_async_copy(source, target, sent.at[len(sends)]))
         sends[-1].start()
 
-    order = grad.shape[0]
+    order = chosen.shape[-1]
     rows = left_stat.shape[0]
     weight = (1.0 - decay) / order
     columns = [slice(n * tile, (n + 1) * tile) for n in range(order // tile)]
@@ -107,6 +113,17 @@
     ]
     for fetch in fetches:
         fetch.start()
+    full, half = chunk.shape[0], far_half.shape[0]
+    row, side = place[1], place[2]
+    far = (row ^ 2) * full
+    for piece, at in (
+        (chunk, row * full),
+        (next_one, (row ^ 1) * full),
+        (last_one, (row ^ 3) * full),
+        (far_half, far + side * half),
+        (far_other, far + (1 - side) * half),
+    ):
+        grad[pl.ds(pl.multiple_of(at, half), piece.shape[0]), :] = piece[...]
     mine = pl.ds(pl.multiple_of(place[0], rows), rows)
     across = ((1,), (0,))
     factor = lax.rsqrt(total[:1] / float(blocks * order * order) + epsilon)
@@ -197,8 +214,8 @@
         copy.wait()
 
 
-def roots(total, due, place, grad, chosen, left_stat, right_stat):
-    order = grad.shape[0]
+def roots(total, due, place, pieces, chosen, left_stat, right_stat):
+    order = chosen.shape[-1]
     tile = 512
     new = jax.ShapeDtypeStruct(left_stat.shape, jnp.float32)
     out = jax.ShapeDtypeStruct(left_stat.shape, jnp.bfloat16)
@@ -209,11 +226,11 @@
     return pl.pallas_call(
         functools.partial(roots_kernel, tile, lax.axis_size(MP)),
         out_shape=(jax.ShapeDtypeStruct((1, order, order), jnp.bfloat16), new, new, out, out),
-        in_specs=[vector, scalar, scalar, vector, far, vector, vector],
+        in_specs=[vector, scalar, scalar, *([vector] * len(pieces)), far, vector, vector],
         out_specs=(far,) * 5,
         scratch_shapes=[
             pltpu.VMEM((2, order, order), jnp.bfloat16),
-            *([square] * 7),
+            *([square] * 8),
             pltpu.VMEM((order, order), jnp.float32),
             pltpu.VMEM((2, *left_stat.shape), jnp.float32),
             pltpu.VMEM((2, *left_stat.shape), jnp.bfloat16),
@@ -223,9 +240,9 @@
         cost_estimate=pl.CostEstimate(
             flops=10 * 2 * order**3, transcendentals=0, bytes_accessed=6 * 2**20
         ),
-        compiler_params=pltpu.CompilerParams(vmem_limit_bytes=44 * 2**20),
+        compiler_params=pltpu.CompilerParams(vmem_limit_bytes=46 * 2**20),
         name="roots",
-    )(total, due, place, grad, chosen, left_stat, right_stat)
+    )(total, due, place, *pieces, chosen, left_stat, right_stat)
 
 
 def per_device(grad_parts, left_stat, right_stat, left_root, right_root, due):
@@ -239,14 +256,22 @@
     part = exchange_sum(partial, WIDE)
     rows = exchange_sum(part, NARROW)
     chunk = spread(rows, ("zl", "zh"))
+    side, row = lax.axis_index("zl"), lax.axis_index("y")
+    middle = chunk.shape[0] // 2
+    own_half = jnp.where(side == 0, chunk[:middle], chunk[middle:])
+    far_half = partner(own_half, "y", 2)
+    next_one = partner(chunk, "y", 1)
+    last_one = partner(chunk, "y", 3)
+    far_other = partner(far_half, "zl", 1)
     squares = jnp.sum(chunk.astype(jnp.float32) ** 2)
     total = jnp.full((8, 128), squares, jnp.float32)
-    for axes in ("c", "x", "y"):
+    for axes in ("c", "x"):
         total = sum_over(total, axes)
-    grad = spread(chunk, "y")
-    place = row_start.astype(jnp.int32).reshape(1)
+    total = sum_over(total, "y")
+    place = jnp.stack([row_start, row, side]).astype(jnp.int32)
+    pieces = (chunk, next_one, last_one, far_half, far_other)
     update, left_new, right_new, left_out, right_out = roots(
-        total, due, place, grad, chosen, left_stat[0], right_stat[0]
+        total, due, place, pieces, chosen, left_stat[0], right_stat[0]
     )
     return (update, left_new[None], right_new[None], left_out[None], right_out[None])
 

time: 143 us -> 148 us (1.035)
  waiting for transfers between devices: 13.5 us -> 36.1 us
  blocking collectives: 74.3 us -> 54.2 us
  starting transfers between devices: 12.9 us -> 15.3 us
    all_to_all x1 -> x0, blocking collectives: 20.2 us -> none  [spread(): parts = lax.all_to_all(copies, axes, 0, 0, tiled=True)]
    all_to_all x1, waiting for transfers between devices: 0.01 us -> 18.1 us  [spread(): parts = lax.all_to_all(copies, axes, 0, 0, tiled=True)]
    ppermute x0 -> x4, waiting for transfers between devices: none -> 5 us  [partner(): return lax.ppermute(value, axis, swap)]
    ppermute x0 -> x4, starting transfers between devices: none -> 3.78 us  [partner(): return lax.ppermute(value, axis, swap)]
  transfers between devices with their start and end apart: 9 -> 13, of which waited for: 5 -> 6; matrix products, arithmetic and copies ran while one was open for 3% -> 3% of each run, Pallas kernels for 0% -> 0%
where the time goes in v4:
time: 148 us
  blocking collectives  54.2 us (37%)
  waiting for transfers between devices  36.1 us (24%)
  Pallas kernels  23.7 us (16%)
  starting transfers between devices  15.3 us (10%)
  between operations  14.2 us (10%)
  other arithmetic  2.69 us (2%)
  local copies, waits for them, and re-layouts  1.52 us (1%)
    all_to_all x2, blocking collectives, exchange_sum(): parts = lax.all_to_all(parts, axes, 0, 0, tiled=True)  54.2 us
    pallas_call x1, Pallas kernels, roots(): pl.pallas_call(functools.partial(roots_kernel, tile, lax.axis_size(MP)),...  22 us
    all_to_all x1, waiting for transfers between devices, spread(): parts = lax.all_to_all(copies, axes, 0, 0, tiled=True)  18.1 us
    ppermute x7, waiting for transfers between devices, sum_over(): parts.append(lax.ppermute(value, axes, swap))  12.9 us
    ppermute x7, starting transfers between devices, sum_over(): parts.append(lax.ppermute(value, axes, swap))  8 us
    ppermute x4, waiting for transfers between devices, partner(): return lax.ppermute(value, axis, swap)  5 us
    ppermute x4, starting transfers between devices, partner(): return lax.ppermute(value, axis, swap)  3.78 us
    all_to_all x1, starting transfers between devices, spread(): parts = lax.all_to_all(copies, axes, 0, 0, tiled=True)  3.49 us
  transfers between devices with their start and end apart: 13, of which 6 were waited for; matrix products, arithmetic and copies ran while one was open for 3% of the time, Pallas kernels for 0%

profile of v4, /device:TPU:2, one launch (start us, length us, event | category | flops | bytes accessed | tf_op | source)
XLA Modules:
  0.0 147.6 jit_solution(3179604173479632274)
XLA Ops:
  7.2 0.0 all-gather.2.cloned.1.call-start
  7.2 1.7 %choose.1 = bf16[2,32,1024]{2,1,0:T(8,128)(2,1)} custom-call(s32[1,2]{1,0:T(1,128)} %refs_1_.1, f32[32,1024]{1,0:T(8,128)} %bitcast.19, f32[32,1024]{1,0:T(8,128)} %bitcast.21, bf16[32,1024]{1,0:T(8,128)(2,1)} %bitcast.26, bf16[32,1024]{1,0:T(8,128)(2,1)} %bitcast.27), custom_call_target="tpu_custom_call" | custom-call | tf_op jit(solution)/shard_map/choose/pallas_call | solution.py:75
  8.9 0.0 all-gather.2.cloned.1.call-update
  9.0 35.7 %all_to_all.15 = bf16[8,128,1024]{2,1,0:T(8,128)(2,1)S(1)} all-to-all(bf16[8,128,1024]{2,1,0:T(8,128)(2,1)} %bitcast.23), channel_id=1, replica_groups=mesh['y'=4,'zh'=4,'zl'=2,'x'=4,'c'=2] {'y','zl'}, dimensions={0} | all-to-all | bytes 4194304 | tf_op jit(solution)/shard_map/all_to_all | solution.py:27
  44.7 0.4 reduce_sum.33
  45.1 0.0 copy-start
  45.1 0.0 copy-start.1
  45.1 0.0 copy-start.2
  45.1 18.5 %all_to_all.16 = bf16[4,32,1024]{2,1,0:T(8,128)(2,1)S(1)} all-to-all(bf16[4,32,1024]{2,1,0:T(8,128)(2,1)S(1)} %bitcast.24), channel_id=1, replica_groups=mesh['y'=4,'zh'=4,'zl'=2,'x'=4,'c'=2] {'zh'}, dimensions={0} | all-to-all | bytes 524288 | tf_op jit(solution)/shard_map/all_to_all | solution.py:27
  63.6 0.9 broadcast_in_dim.21
  64.5 3.5 %all-to-all-start.2 = ((bf16[8,32,1024]{2,1,0:T(8,128)(2,1)}), bf16[8,32,1024]{2,1,0:T(8,128)(2,1)S(1)}, u32[]{:S(2)}, u32[]{:S(2)}) async-start(bf16[8,32,1024]{2,1,0:T(8,128)(2,1)} %broadcast_in_dim.21), calls=%async_computation.2 | async-start | bytes 1048576 | tf_op jit(solution)/shard_map/all_to_all | solution.py:34
  68.0 18.1 %all-to-all-done.2 = bf16[8,32,1024]{2,1,0:T(8,128)(2,1)S(1)} async-done(((bf16[8,32,1024]{2,1,0:T(8,128)(2,1)}), bf16[8,32,1024]{2,1,0:T(8,128)(2,1)S(1)}, u32[]{:S(2)}, u32[]{:S(2)}) %all-to-all-start.2) | async-done | bytes 524320 | tf_op jit(solution)/shard_map/all_to_all | solution.py:34
  86.1 0.9 multiply_reduce_fusion
  86.9 0.6 broadcast_in_dim.22
  87.6 0.1 collective-permute-start
  87.7 0.1 collective-permute-start.9
  87.8 1.0 collective-permute-done
  88.9 0.6 broadcast_add_fusion
  89.5 2.3 %collective-permute-start.2 = (f32[8,128]{1,0:T(8,128)S(1)}, f32[8,128]{1,0:T(8,128)S(1)}, u32[]{:S(2)}, u32[]{:S(2)}) collective-permute-start(f32[8,128]{1,0:T(8,128)S(1)} %broadcast_add_fusion), channel_id=1, source_target_pairs={{0,4},{2,6},{4,0},{6,2},{1,5},{3,7},{5,1},{7,3},{8,12},{10,14},{12... | collective-permute-start | bytes 12296 | tf_op jit(solution)/shard_map/ppermute | solution.py:43
  91.8 0.0 collective-permute-start.3
  91.8 2.5 %collective-permute-start.1 = (f32[8,128]{1,0:T(8,128)S(1)}, f32[8,128]{1,0:T(8,128)S(1)}, u32[]{:S(2)}, u32[]{:S(2)}) collective-permute-start(f32[8,128]{1,0:T(8,128)S(1)} %broadcast_add_fusion), channel_id=1, source_target_pairs={{0,2},{2,0},{4,6},{6,4},{1,3},{3,1},{5,7},{7,5},{8,10},{10,8},{12,... | collective-permute-start | bytes 12296 | tf_op jit(solution)/shard_map/ppermute | solution.py:43
  94.3 0.1 collective-permute-start.8
  94.4 0.3 collective-permute-done.2
  94.7 2.1 %collective-permute-start.7 = (bf16[256,1024]{1,0:T(8,128)(2,1)S(1)}, bf16[256,1024]{1,0:T(8,128)(2,1)S(1)}, u32[]{:S(2)}, u32[]{:S(2)}) collective-permute-start(bf16[256,1024]{1,0:T(8,128)(2,1)S(1)} %bitcast.17), channel_id=1, source_target_pairs={{0,64},{64,0},{128,192},{192,128},{1,65},{65,1},{129,193},{193,129... | collective-permute-start | bytes 1572872 | tf_op jit(solution)/shard_map/ppermute | solution.py:51
  96.8 0.0 collective-permute-done.3
  96.8 0.0 collective-permute-done.1
  96.8 0.7 add_add_fusion.1
  97.4 1.1 collective-permute-start.6
  98.5 1.3 collective-permute-start.5
  99.9 10.3 %collective-permute-done.6 = f32[8,128]{1,0:T(8,128)S(1)} collective-permute-done((f32[8,128]{1,0:T(8,128)S(1)}, f32[8,128]{1,0:T(8,128)S(1)}, u32[]{:S(2)}, u32[]{:S(2)}) %collective-permute-start.6) | collective-permute-done | bytes 4128 | tf_op jit(solution)/shard_map/ppermute | solution.py:43
  110.2 0.7 collective-permute-start.4
  110.9 0.0 collective-permute-done.9.refs_6_
  110.9 1.5 %collective-permute-start.10 = (bf16[128,1024]{1,0:T(8,128)(2,1)S(1)}, bf16[128,1024]{1,0:T(8,128)(2,1)S(1)}, u32[]{:S(2)}, u32[]{:S(2)}) collective-permute-start(bf16[128,1024]{1,0:T(8,128)(2,1)S(1)} %collective-permute-done.9.refs_6_), channel_id=1, source_target_pairs={{0,8},{8,0},{1,9},{9,1},{2,10},{10,2},{3,11},{11,3},{4,12},{12,4},... | collective-permute-start | bytes 786440 | tf_op jit(solution)/shard_map/ppermute | solution.py:51
  112.3 0.1 pad_add_fusion.refs_2_
  112.4 0.0 collective-permute-done.5
  112.4 1.4 collective-permute-done.4
  113.8 0.0 collective-permute-done.8.refs_5_
  113.8 0.0 collective-permute-done.7.refs_4_
  113.8 5.0 %collective-permute-done.10.refs_7_ = bf16[128,1024]{1,0:T(8,128)(2,1)S(1)} collective-permute-done((bf16[128,1024]{1,0:T(8,128)(2,1)S(1)}, bf16[128,1024]{1,0:T(8,128)(2,1)S(1)}, u32[]{:S(2)}, u32[]{:S(2)}) %collective-permute-start.10) | collective-permute-done | bytes 262176 | tf_op jit(solution)/shard_map/ppermute | solution.py:51
  118.8 0.0 all-gather.2.cloned.1.call-done.refs_8_
  118.8 0.0 copy-done
  118.8 0.0 copy-done.1
  118.8 0.0 copy-done.2
  118.8 22.0 %roots.1 = (bf16[1,1024,1024]{2,1,0:T(8,128)(2,1)}, f32[32,1024]{1,0:T(8,128)}, f32[32,1024]{1,0:T(8,128)}, bf16[32,1024]{1,0:T(8,128)(2,1)}, bf16[32,1024]{1,0:T(8,128)(2,1)}) custom-call(f32[8,128]{1,0:T(8,128)S(1)} %add_add_fusion.refs_0_, s32[1,2]{1,0:T(1,128)S(1)} %copy-done.2, s32[3]{0:T(128)S(1)} %pad_add_fusion.refs_2_, ...), custom_call_target="tpu_custom_call" | custom-call | flops 21474836480 | bytes 6291456 | tf_op jit(solution)/shard_map/roots/pallas_call | solution.py:226
  (3 shorter events, 0.1 us)
Async XLA Ops:
  7.2 111.6 %all-gather.2.cloned.1.call-start = ((), (), s32[]{:S(2)}) async-start(), calls=%async_computation.3 | async-start | bytes 4325376 | tf_op jit(solution)/shard_map/all_gather | solution.py:253
  45.1 73.7 %copy-start = (f32[1,32,1024]{2,1,0:T(8,128)S(1)}, f32[1,32,1024]{2,1,0:T(8,128)}, u32[]{:S(2)}) copy-start(f32[1,32,1024]{2,1,0:T(8,128)} %param.7) | copy-start | bytes 393220
  45.1 73.7 %copy-start.1 = (f32[1,32,1024]{2,1,0:T(8,128)S(1)}, f32[1,32,1024]{2,1,0:T(8,128)}, u32[]{:S(2)}) copy-start(f32[1,32,1024]{2,1,0:T(8,128)} %param.8) | copy-start | bytes 393220
  45.1 73.7 %copy-start.2 = (s32[1,2]{1,0:T(1,128)S(1)}, s32[1,2]{1,0:T(1,128)}, u32[]{:S(2)}) copy-start(s32[1,2]{1,0:T(1,128)} %refs_1_.1) | copy-start | bytes 28
  64.5 21.6 %all-to-all-start.2 = ((bf16[8,32,1024]{2,1,0:T(8,128)(2,1)}), bf16[8,32,1024]{2,1,0:T(8,128)(2,1)S(1)}, u32[]{:S(2)}, u32[]{:S(2)}) async-start(bf16[8,32,1024]{2,1,0:T(8,128)(2,1)} %broadcast_in_dim.21), calls=%async_computation.2 | async-start | bytes 1048576 | tf_op jit(solution)/shard_map/all_to_all | solution.py:34
  87.6 1.3 collective-permute-start
  87.7 23.1 %collective-permute-start.9 = (bf16[128,1024]{1,0:T(8,128)(2,1)S(1)}, bf16[128,1024]{1,0:T(8,128)(2,1)S(1)}, u32[]{:S(2)}, u32[]{:S(2)}) collective-permute-start(bf16[128,1024]{1,0:T(8,128)(2,1)S(1)} %bitcast.25), channel_id=1, source_target_pairs={{0,128},{64,192},{128,0},{192,64},{1,129},{65,193},{129,1},{193,65... | collective-permute-start | bytes 786440 | tf_op jit(solution)/shard_map/ppermute | solution.py:51
  89.5 5.2 %collective-permute-start.2 = (f32[8,128]{1,0:T(8,128)S(1)}, f32[8,128]{1,0:T(8,128)S(1)}, u32[]{:S(2)}, u32[]{:S(2)}) collective-permute-start(f32[8,128]{1,0:T(8,128)S(1)} %broadcast_add_fusion), channel_id=1, source_target_pairs={{0,4},{2,6},{4,0},{6,2},{1,5},{3,7},{5,1},{7,3},{8,12},{10,14},{12... | collective-permute-start | bytes 12296 | tf_op jit(solution)/shard_map/ppermute | solution.py:43
  91.8 4.9 %collective-permute-start.3 = (f32[8,128]{1,0:T(8,128)S(1)}, f32[8,128]{1,0:T(8,128)S(1)}, u32[]{:S(2)}, u32[]{:S(2)}) collective-permute-start(f32[8,128]{1,0:T(8,128)S(1)} %broadcast_add_fusion), channel_id=1, source_target_pairs={{0,6},{2,4},{4,2},{6,0},{1,7},{3,5},{5,3},{7,1},{8,14},{10,12},{12... | collective-permute-start | bytes 12296 | tf_op jit(solution)/shard_map/ppermute | solution.py:43
  91.8 4.9 %collective-permute-start.1 = (f32[8,128]{1,0:T(8,128)S(1)}, f32[8,128]{1,0:T(8,128)S(1)}, u32[]{:S(2)}, u32[]{:S(2)}) collective-permute-start(f32[8,128]{1,0:T(8,128)S(1)} %broadcast_add_fusion), channel_id=1, source_target_pairs={{0,2},{2,0},{4,6},{6,4},{1,3},{3,1},{5,7},{7,5},{8,10},{10,8},{12,... | collective-permute-start | bytes 12296 | tf_op jit(solution)/shard_map/ppermute | solution.py:43
  94.3 19.5 %collective-permute-start.8 = (bf16[256,1024]{1,0:T(8,128)(2,1)S(1)}, bf16[256,1024]{1,0:T(8,128)(2,1)S(1)}, u32[]{:S(2)}, u32[]{:S(2)}) collective-permute-start(bf16[256,1024]{1,0:T(8,128)(2,1)S(1)} %bitcast.16), channel_id=1, source_target_pairs={{0,192},{64,128},{128,64},{192,0},{1,193},{65,129},{129,65},{193,1... | collective-permute-start | bytes 1572872 | tf_op jit(solution)/shard_map/ppermute | solution.py:51
  94.7 19.1 %collective-permute-start.7 = (bf16[256,1024]{1,0:T(8,128)(2,1)S(1)}, bf16[256,1024]{1,0:T(8,128)(2,1)S(1)}, u32[]{:S(2)}, u32[]{:S(2)}) collective-permute-start(bf16[256,1024]{1,0:T(8,128)(2,1)S(1)} %bitcast.17), channel_id=1, source_target_pairs={{0,64},{64,0},{128,192},{192,128},{1,65},{65,1},{129,193},{193,129... | collective-permute-start | bytes 1572872 | tf_op jit(solution)/shard_map/ppermute | solution.py:51
  97.4 12.7 %collective-permute-start.6 = (f32[8,128]{1,0:T(8,128)S(1)}, f32[8,128]{1,0:T(8,128)S(1)}, u32[]{:S(2)}, u32[]{:S(2)}) collective-permute-start(f32[8,128]{1,0:T(8,128)S(1)} %add_add_fusion.1), channel_id=1, source_target_pairs={{0,192},{64,128},{128,64},{192,0},{1,193},{65,129},{129,65},{193,1... | collective-permute-start | bytes 12296 | tf_op jit(solution)/shard_map/ppermute | solution.py:43
  98.5 13.9 %collective-permute-start.5 = (f32[8,128]{1,0:T(8,128)S(1)}, f32[8,128]{1,0:T(8,128)S(1)}, u32[]{:S(2)}, u32[]{:S(2)}) collective-permute-start(f32[8,128]{1,0:T(8,128)S(1)} %add_add_fusion.1), channel_id=1, source_target_pairs={{0,128},{64,192},{128,0},{192,64},{1,129},{65,193},{129,1},{193,65... | collective-permute-start | bytes 12296 | tf_op jit(solution)/shard_map/ppermute | solution.py:43
  110.2 3.6 %collective-permute-start.4 = (f32[8,128]{1,0:T(8,128)S(1)}, f32[8,128]{1,0:T(8,128)S(1)}, u32[]{:S(2)}, u32[]{:S(2)}) collective-permute-start(f32[8,128]{1,0:T(8,128)S(1)} %add_add_fusion.1), channel_id=1, source_target_pairs={{0,64},{64,0},{128,192},{192,128},{1,65},{65,1},{129,193},{193,129... | collective-permute-start | bytes 12296 | tf_op jit(solution)/shard_map/ppermute | solution.py:43
  110.9 7.9 %collective-permute-start.10 = (bf16[128,1024]{1,0:T(8,128)(2,1)S(1)}, bf16[128,1024]{1,0:T(8,128)(2,1)S(1)}, u32[]{:S(2)}, u32[]{:S(2)}) collective-permute-start(bf16[128,1024]{1,0:T(8,128)(2,1)S(1)} %collective-permute-done.9.refs_6_), channel_id=1, source_target_pairs={{0,8},{8,0},{1,9},{9,1},{2,10},{10,2},{3,11},{11,3},{4,12},{12,4},... | collective-permute-start | bytes 786440 | tf_op jit(solution)/shard_map/ppermute | solution.py:51
Sparse Core Ops, SparseCore 0:
  11.1 92.3 all-gather.1

commit v5 on v4

--- a/solution.py
+++ b/solution.py
@@ -51,7 +51,7 @@
     return lax.ppermute(value, axis, swap)
 
 
-def choose_kernel(due, left_stat, right_stat, left_root, right_root, chosen, *scratch):
+def choose_kernel(index, due, left_stat, right_stat, left_root, right_root, chosen, *scratch):
     flags, *held, sems = scratch
     far = (due, left_stat, right_stat, left_root, right_root)
     fetches = [
@@ -67,7 +67,7 @@
         chosen[k] = jnp.where(flags[0, k] == 1, stat.astype(jnp.bfloat16), root)
 
 
-def choose(*arrays):
+def choose(index, *arrays):
     far = pl.BlockSpec(memory_space=pltpu.HBM)
     arrays = [pltpu.with_memory_space_constraint(a, pltpu.HBM) for a in arrays]
     due, *rows = arrays
@@ -75,7 +75,7 @@
     return pl.pallas_call(
         choose_kernel,
         out_shape=jax.ShapeDtypeStruct((2, *root.shape), root.dtype),
-        in_specs=[far] * len(arrays),
+        in_specs=[pl.BlockSpec(memory_space=pltpu.SMEM), *([far] * len(arrays))],
         out_specs=pl.BlockSpec(memory_space=pltpu.VMEM),
         scratch_shapes=[
             pltpu.SMEM(due.shape, due.dtype),
@@ -84,11 +84,38 @@
         ],
         compiler_params=pltpu.CompilerParams(vmem_limit_bytes=4 * 2**20),
         name="choose",
-    )(*arrays)
+    )(index, *arrays)
+
+
+def halve_kernel(index, chunk, half, squares):
+    rows = half.shape[0]
+    side = index[0] % 2
+    half[...] = chunk[pl.ds(pl.multiple_of(side * rows, rows), rows), :]
+    total = jnp.zeros((32, chunk.shape[1]), jnp.float32)
+    for i in range(0, chunk.shape[0], 32):
+        part = chunk[i : i + 32, :].astype(jnp.float32)
+        total = total + part * part
+    squares[...] = jnp.full(squares.shape, jnp.sum(total), jnp.float32)
+
+
+def halve(index, chunk):
+    rows, order = chunk.shape
+    vector = pl.BlockSpec(memory_space=pltpu.VMEM)
+    return pl.pallas_call(
+        halve_kernel,
+        out_shape=(
+            jax.ShapeDtypeStruct((rows // 2, order), chunk.dtype),
+            jax.ShapeDtypeStruct((8, 128), jnp.float32),
+        ),
+        in_specs=[pl.BlockSpec(memory_space=pltpu.SMEM), vector],
+        out_specs=(vector, vector),
+        compiler_params=pltpu.CompilerParams(vmem_limit_bytes=4 * 2**20),
+        name="halve",
+    )(index, chunk)
 
 
 def roots_kernel(tile, blocks, *refs):
-    total, due, place = refs[:3]
+    total, due, index = refs[:3]
     chunk, next_one, last_one, far_half, far_other, chosen, left_stat, right_stat = refs[3:11]
     update, left_new, right_new, left_out, right_out = refs[11:16]
     picked, grad, flipped, first, second, mixed, used, x, fourth, block = refs[16:26]
@@ -114,7 +141,7 @@
     for fetch in fetches:
         fetch.start()
     full, half = chunk.shape[0], far_half.shape[0]
-    row, side = place[1], place[2]
+    row, side = index[0] // 8, index[0] % 2
     far = (row ^ 2) * full
     for piece, at in (
         (chunk, row * full),
@@ -124,7 +151,7 @@
         (far_other, far + (1 - side) * half),
     ):
         grad[pl.ds(pl.multiple_of(at, half), piece.shape[0]), :] = piece[...]
-    mine = pl.ds(pl.multiple_of(place[0], rows), rows)
+    mine = pl.ds(pl.multiple_of(index[0] * rows, rows), rows)
     across = ((1,), (0,))
     factor = lax.rsqrt(total[:1] / float(blocks * order * order) + epsilon)
     factor = jnp.broadcast_to(factor[:, :1], (1, tile))
@@ -214,7 +241,7 @@
         copy.wait()
 
 
-def roots(total, due, place, pieces, chosen, left_stat, right_stat):
+def roots(total, due, index, pieces, chosen, left_stat, right_stat):
     order = chosen.shape[-1]
     tile = 512
     new = jax.ShapeDtypeStruct(left_stat.shape, jnp.float32)
@@ -242,13 +269,12 @@
         ),
         compiler_params=pltpu.CompilerParams(vmem_limit_bytes=46 * 2**20),
         name="roots",
-    )(total, due, place, *pieces, chosen, left_stat, right_stat)
+    )(total, due, index, *pieces, chosen, left_stat, right_stat)
 
 
 def per_device(grad_parts, left_stat, right_stat, left_root, right_root, due):
-    row_count = left_stat.shape[1]
-    row_start = lax.axis_index(DP) * row_count
-    chosen = choose(due, left_stat[0], right_stat[0], left_root[0], right_root[0])
+    index = lax.axis_index(DP).astype(jnp.int32).reshape(1)
+    chosen = choose(index, due, left_stat[0], right_stat[0], left_root[0], right_root[0])
     chosen, partial = lax.optimization_barrier((chosen, grad_parts[0, 0]))
     chosen = lax.all_gather(chosen, DP, axis=1, tiled=True)
     chosen = pltpu.with_memory_space_constraint(chosen, pltpu.HBM)
@@ -256,22 +282,17 @@
     part = exchange_sum(partial, WIDE)
     rows = exchange_sum(part, NARROW)
     chunk = spread(rows, ("zl", "zh"))
-    side, row = lax.axis_index("zl"), lax.axis_index("y")
-    middle = chunk.shape[0] // 2
-    own_half = jnp.where(side == 0, chunk[:middle], chunk[middle:])
+    own_half, total = halve(index, chunk)
     far_half = partner(own_half, "y", 2)
     next_one = partner(chunk, "y", 1)
     last_one = partner(chunk, "y", 3)
+    total = sum_over(total, "c")
     far_other = partner(far_half, "zl", 1)
-    squares = jnp.sum(chunk.astype(jnp.float32) ** 2)
-    total = jnp.full((8, 128), squares, jnp.float32)
-    for axes in ("c", "x"):
-        total = sum_over(total, axes)
+    total = sum_over(total, "x")
     total = sum_over(total, "y")
-    place = jnp.stack([row_start, row, side]).astype(jnp.int32)
     pieces = (chunk, next_one, last_one, far_half, far_other)
     update, left_new, right_new, left_out, right_out = roots(
-        total, due, place, pieces, chosen, left_stat[0], right_stat[0]
+        total, due, index, pieces, chosen, left_stat[0], right_stat[0]
     )
     return (update, left_new[None], right_new[None], left_out[None], right_out[None])
 

time: 148 us -> 139 us (0.939)
  waiting for transfers between devices: 36.1 us -> 13.8 us
  blocking collectives: 54.2 us -> 74.6 us
  starting transfers between devices: 15.3 us -> 10.7 us
  other arithmetic: 2.69 us -> 0.42 us
    all_to_all x0 -> x1, blocking collectives: none -> 20.4 us  [spread(): parts = lax.all_to_all(copies, axes, 0, 0, tiled=True)]
    all_to_all x1 -> x0, waiting for transfers between devices: 18.1 us -> none  [spread(): parts = lax.all_to_all(copies, axes, 0, 0, tiled=True)]
    all_to_all x1 -> x0, starting transfers between devices: 3.49 us -> none  [spread(): parts = lax.all_to_all(copies, axes, 0, 0, tiled=True)]
    ppermute x7, waiting for transfers between devices: 12.9 us -> 9.51 us  [sum_over(): parts.append(lax.ppermute(value, axes, swap))]
  transfers between devices with their start and end apart: 13 -> 12, of which waited for: 6 -> 6; matrix products, arithmetic and copies ran while one was open for 3% -> 0% of each run, Pallas kernels for 0% -> 0%
where the time goes in v5:
time: 139 us; the launch traced here: 138 us
  blocking collectives  74.6 us (54%)
  Pallas kernels  23.9 us (17%)
  between operations  14.2 us (10%)
  waiting for transfers between devices  13.8 us (10%)
  starting transfers between devices  10.7 us (8%)
    all_to_all x2, blocking collectives, exchange_sum(): parts = lax.all_to_all(parts, axes, 0, 0, tiled=True)  54.2 us
    pallas_call x1, Pallas kernels, roots(): pl.pallas_call(functools.partial(roots_kernel, tile, lax.axis_size(MP)),...  22 us
    all_to_all x1, blocking collectives, spread(): parts = lax.all_to_all(copies, axes, 0, 0, tiled=True)  20.4 us
    ppermute x7, waiting for transfers between devices, sum_over(): parts.append(lax.ppermute(value, axes, swap))  9.51 us
    ppermute x7, starting transfers between devices, sum_over(): parts.append(lax.ppermute(value, axes, swap))  6.71 us
    ppermute x4, waiting for transfers between devices, partner(): return lax.ppermute(value, axis, swap)  4.3 us
    ppermute x4, starting transfers between devices, partner(): return lax.ppermute(value, axis, swap)  3.98 us
  transfers between devices with their start and end apart: 12, of which 6 were waited for; matrix products, arithmetic and copies ran while one was open for 0% of the time, Pallas kernels for 0%

profile of v5, /device:TPU:2, one launch (start us, length us, event | category | flops | bytes accessed | tf_op | source)
XLA Modules:
  0.0 137.7 jit_solution(13636526672802135926)
XLA Ops:
  7.2 0.0 all-gather.2.cloned.1.call-start
  7.2 1.7 %choose.1 = bf16[2,32,1024]{2,1,0:T(8,128)(2,1)} custom-call(s32[1]{0:T(128)} %bitcast.index.refs_2_, s32[1,2]{1,0:T(1,128)} %refs_1_.1, f32[32,1024]{1,0:T(8,128)} %bitcast.17, f32[32,1024]{1,0:T(8,128)} %bitcast.19, bf16[32,1024]{1,0:T(8,128)(2,1)} %bitcast.23, bf16[32,1024]{1,0:T(8,128)(2,1)} %bitcast.24), custom_call_target="tpu_custom_call" | custom-call | tf_op jit(solution)/shard_map/choose/pallas_call | solution.py:75
  8.9 0.0 all-gather.2.cloned.1.call-update
  9.0 35.7 %all_to_all.15 = bf16[8,128,1024]{2,1,0:T(8,128)(2,1)S(1)} all-to-all(bf16[8,128,1024]{2,1,0:T(8,128)(2,1)} %bitcast.21), channel_id=1, replica_groups=mesh['y'=4,'zh'=4,'zl'=2,'x'=4,'c'=2] {'y','zl'}, dimensions={0} | all-to-all | bytes 4194304 | tf_op jit(solution)/shard_map/all_to_all | solution.py:27
  44.7 0.4 reduce_sum.24
  45.1 0.0 copy-start
  45.1 0.0 copy-start.1
  45.1 0.0 copy-start.2
  45.1 18.5 %all_to_all.16 = bf16[4,32,1024]{2,1,0:T(8,128)(2,1)S(1)} all-to-all(bf16[4,32,1024]{2,1,0:T(8,128)(2,1)S(1)} %bitcast.22), channel_id=1, replica_groups=mesh['y'=4,'zh'=4,'zl'=2,'x'=4,'c'=2] {'zh'}, dimensions={0} | all-to-all | bytes 524288 | tf_op jit(solution)/shard_map/all_to_all | solution.py:27
  63.6 0.1 broadcast_in_dim.18
  63.7 20.4 %all_to_all.17 = bf16[8,32,1024]{2,1,0:T(8,128)(2,1)S(1)} all-to-all(bf16[8,32,1024]{2,1,0:T(8,128)(2,1)S(1)} %broadcast_in_dim.18), channel_id=1, replica_groups=mesh['y'=4,'zh'=4,'zl'=2,'x'=4,'c'=2] {'zl','zh'}, dimensions={0} | all-to-all | bytes 1048576 | tf_op jit(solution)/shard_map/all_to_all | solution.py:34
  84.0 0.2 halve.1
  84.3 0.1 collective-permute-start.9
  84.4 0.6 collective-permute-start.8
  84.9 2.9 %collective-permute-start.7 = (bf16[256,1024]{1,0:T(8,128)(2,1)S(1)}, bf16[256,1024]{1,0:T(8,128)(2,1)S(1)}, u32[]{:S(2)}, u32[]{:S(2)}) collective-permute-start(bf16[256,1024]{1,0:T(8,128)(2,1)S(1)} %bitcast.15), channel_id=1, source_target_pairs={{0,64},{64,0},{128,192},{192,128},{1,65},{65,1},{129,193},{193,129... | collective-permute-start | bytes 1572872 | tf_op jit(solution)/shard_map/ppermute | solution.py:51
  87.9 0.0 collective-permute-start
  87.9 1.2 collective-permute-done
  89.0 1.5 %collective-permute-start.3 = (f32[8,128]{1,0:T(8,128)S(1)}, f32[8,128]{1,0:T(8,128)S(1)}, u32[]{:S(2)}, u32[]{:S(2)}) collective-permute-start(f32[8,128]{1,0:T(8,128)S(1)} %add.29), channel_id=1, source_target_pairs={{0,6},{2,4},{4,2},{6,0},{1,7},{3,5},{5,3},{7,1},{8,14},{10,12},{12... | collective-permute-start | bytes 12296 | tf_op jit(solution)/shard_map/ppermute | solution.py:43
  90.5 0.9 collective-permute-start.2
  91.4 1.2 collective-permute-done.3
  92.6 1.5 %collective-permute-start.1 = (f32[8,128]{1,0:T(8,128)S(1)}, f32[8,128]{1,0:T(8,128)S(1)}, u32[]{:S(2)}, u32[]{:S(2)}) collective-permute-start(f32[8,128]{1,0:T(8,128)S(1)} %add.29), channel_id=1, source_target_pairs={{0,2},{2,0},{4,6},{6,4},{1,3},{3,1},{5,7},{7,5},{8,10},{10,8},{12,... | collective-permute-start | bytes 12296 | tf_op jit(solution)/shard_map/ppermute | solution.py:43
  94.2 4.3 %collective-permute-done.9.refs_6_ = bf16[128,1024]{1,0:T(8,128)(2,1)S(1)} collective-permute-done((bf16[128,1024]{1,0:T(8,128)(2,1)S(1)}, bf16[128,1024]{1,0:T(8,128)(2,1)S(1)}, u32[]{:S(2)}, u32[]{:S(2)}) %collective-permute-start.9) | collective-permute-done | bytes 262176 | tf_op jit(solution)/shard_map/ppermute | solution.py:51
  98.5 0.4 collective-permute-start.10
  98.9 0.0 collective-permute-done.2
  98.9 0.0 collective-permute-done.1
  98.9 1.2 collective-permute-start.6
  100.1 1.6 %collective-permute-start.5 = (f32[8,128]{1,0:T(8,128)S(1)}, f32[8,128]{1,0:T(8,128)S(1)}, u32[]{:S(2)}, u32[]{:S(2)}) collective-permute-start(f32[8,128]{1,0:T(8,128)S(1)} %add_add_fusion.1), channel_id=1, source_target_pairs={{0,128},{64,192},{128,0},{192,64},{1,129},{65,193},{129,1},{193,65... | collective-permute-start | bytes 12296 | tf_op jit(solution)/shard_map/ppermute | solution.py:43
  101.7 3.5 %collective-permute-done.6 = f32[8,128]{1,0:T(8,128)S(1)} collective-permute-done((f32[8,128]{1,0:T(8,128)S(1)}, f32[8,128]{1,0:T(8,128)S(1)}, u32[]{:S(2)}, u32[]{:S(2)}) %collective-permute-start.6) | collective-permute-done | bytes 4128 | tf_op jit(solution)/shard_map/ppermute | solution.py:43
  105.2 0.0 collective-permute-start.4
  105.2 0.2 collective-permute-done.5
  105.4 3.4 %collective-permute-done.4 = f32[8,128]{1,0:T(8,128)S(1)} collective-permute-done((f32[8,128]{1,0:T(8,128)S(1)}, f32[8,128]{1,0:T(8,128)S(1)}, u32[]{:S(2)}, u32[]{:S(2)}) %collective-permute-start.4) | collective-permute-done | bytes 4128 | tf_op jit(solution)/shard_map/ppermute | solution.py:43
  108.8 0.0 collective-permute-done.8.refs_5_
  108.8 0.0 collective-permute-done.7.refs_4_
  108.8 0.0 collective-permute-done.10.refs_7_
  108.8 0.0 all-gather.2.cloned.1.call-done.refs_8_
  108.9 0.0 copy-done
  108.9 0.0 copy-done.1
  108.9 0.0 copy-done.2
  108.9 22.0 %roots.1 = (bf16[1,1024,1024]{2,1,0:T(8,128)(2,1)}, f32[32,1024]{1,0:T(8,128)}, f32[32,1024]{1,0:T(8,128)}, bf16[32,1024]{1,0:T(8,128)(2,1)}, bf16[32,1024]{1,0:T(8,128)(2,1)}) custom-call(f32[8,128]{1,0:T(8,128)S(1)} %add_add_fusion.refs_0_, s32[1,2]{1,0:T(1,128)S(1)} %copy-done.2, s32[1]{0:T(128)} %bitcast.index.refs_2_, bf16[256,1024]{1,0:T(8,128)(2,1)S(1)} %bitcast.16, ...), custom_call_target="tpu_custom_call" | custom-call | flops 21474836480 | bytes 6291456 | tf_op jit(solution)/shard_map/roots/pallas_call | solution.py:253
  (4 shorter events, 0.1 us)
Async XLA Ops:
  7.2 101.7 %all-gather.2.cloned.1.call-start = ((), (), s32[]{:S(2)}) async-start(), calls=%async_computation.3 | async-start | bytes 4325376 | tf_op jit(solution)/shard_map/all_gather | solution.py:279
  45.1 63.8 %copy-start = (f32[1,32,1024]{2,1,0:T(8,128)S(1)}, f32[1,32,1024]{2,1,0:T(8,128)}, u32[]{:S(2)}) copy-start(f32[1,32,1024]{2,1,0:T(8,128)} %param.7) | copy-start | bytes 393220
  45.1 63.8 %copy-start.1 = (f32[1,32,1024]{2,1,0:T(8,128)S(1)}, f32[1,32,1024]{2,1,0:T(8,128)}, u32[]{:S(2)}) copy-start(f32[1,32,1024]{2,1,0:T(8,128)} %param.8) | copy-start | bytes 393220
  45.1 63.8 %copy-start.2 = (s32[1,2]{1,0:T(1,128)S(1)}, s32[1,2]{1,0:T(1,128)}, u32[]{:S(2)}) copy-start(s32[1,2]{1,0:T(1,128)} %refs_1_.1) | copy-start | bytes 28
  84.3 14.2 %collective-permute-start.9 = (bf16[128,1024]{1,0:T(8,128)(2,1)S(1)}, bf16[128,1024]{1,0:T(8,128)(2,1)S(1)}, u32[]{:S(2)}, u32[]{:S(2)}) collective-permute-start(bf16[128,1024]{1,0:T(8,128)(2,1)S(1)} %get-tuple-element.16), channel_id=1, source_target_pairs={{0,128},{64,192},{128,0},{192,64},{1,129},{65,193},{129,1},{193,65... | collective-permute-start | bytes 786440 | tf_op jit(solution)/shard_map/ppermute | solution.py:51
  84.4 24.4 %collective-permute-start.8 = (bf16[256,1024]{1,0:T(8,128)(2,1)S(1)}, bf16[256,1024]{1,0:T(8,128)(2,1)S(1)}, u32[]{:S(2)}, u32[]{:S(2)}) collective-permute-start(bf16[256,1024]{1,0:T(8,128)(2,1)S(1)} %bitcast.14), channel_id=1, source_target_pairs={{0,192},{64,128},{128,64},{192,0},{1,193},{65,129},{129,65},{193,1... | collective-permute-start | bytes 1572872 | tf_op jit(solution)/shard_map/ppermute | solution.py:51
  84.9 23.9 %collective-permute-start.7 = (bf16[256,1024]{1,0:T(8,128)(2,1)S(1)}, bf16[256,1024]{1,0:T(8,128)(2,1)S(1)}, u32[]{:S(2)}, u32[]{:S(2)}) collective-permute-start(bf16[256,1024]{1,0:T(8,128)(2,1)S(1)} %bitcast.15), channel_id=1, source_target_pairs={{0,64},{64,0},{128,192},{192,128},{1,65},{65,1},{129,193},{193,129... | collective-permute-start | bytes 1572872 | tf_op jit(solution)/shard_map/ppermute | solution.py:51
  87.9 1.2 collective-permute-start
  89.0 3.6 %collective-permute-start.3 = (f32[8,128]{1,0:T(8,128)S(1)}, f32[8,128]{1,0:T(8,128)S(1)}, u32[]{:S(2)}, u32[]{:S(2)}) collective-permute-start(f32[8,128]{1,0:T(8,128)S(1)} %add.29), channel_id=1, source_target_pairs={{0,6},{2,4},{4,2},{6,0},{1,7},{3,5},{5,3},{7,1},{8,14},{10,12},{12... | collective-permute-start | bytes 12296 | tf_op jit(solution)/shard_map/ppermute | solution.py:43
  90.5 8.3 %collective-permute-start.2 = (f32[8,128]{1,0:T(8,128)S(1)}, f32[8,128]{1,0:T(8,128)S(1)}, u32[]{:S(2)}, u32[]{:S(2)}) collective-permute-start(f32[8,128]{1,0:T(8,128)S(1)} %add.29), channel_id=1, source_target_pairs={{0,4},{2,6},{4,0},{6,2},{1,5},{3,7},{5,1},{7,3},{8,12},{10,14},{12... | collective-permute-start | bytes 12296 | tf_op jit(solution)/shard_map/ppermute | solution.py:43
  92.6 6.2 %collective-permute-start.1 = (f32[8,128]{1,0:T(8,128)S(1)}, f32[8,128]{1,0:T(8,128)S(1)}, u32[]{:S(2)}, u32[]{:S(2)}) collective-permute-start(f32[8,128]{1,0:T(8,128)S(1)} %add.29), channel_id=1, source_target_pairs={{0,2},{2,0},{4,6},{6,4},{1,3},{3,1},{5,7},{7,5},{8,10},{10,8},{12,... | collective-permute-start | bytes 12296 | tf_op jit(solution)/shard_map/ppermute | solution.py:43
  98.5 10.4 %collective-permute-start.10 = (bf16[128,1024]{1,0:T(8,128)(2,1)S(1)}, bf16[128,1024]{1,0:T(8,128)(2,1)S(1)}, u32[]{:S(2)}, u32[]{:S(2)}) collective-permute-start(bf16[128,1024]{1,0:T(8,128)(2,1)S(1)} %collective-permute-done.9.refs_6_), channel_id=1, source_target_pairs={{0,8},{8,0},{1,9},{9,1},{2,10},{10,2},{3,11},{11,3},{4,12},{12,4},... | collective-permute-start | bytes 786440 | tf_op jit(solution)/shard_map/ppermute | solution.py:51
  98.9 6.3 %collective-permute-start.6 = (f32[8,128]{1,0:T(8,128)S(1)}, f32[8,128]{1,0:T(8,128)S(1)}, u32[]{:S(2)}, u32[]{:S(2)}) collective-permute-start(f32[8,128]{1,0:T(8,128)S(1)} %add_add_fusion.1), channel_id=1, source_target_pairs={{0,192},{64,128},{128,64},{192,0},{1,193},{65,129},{129,65},{193,1... | collective-permute-start | bytes 12296 | tf_op jit(solution)/shard_map/ppermute | solution.py:43
  100.1 5.3 %collective-permute-start.5 = (f32[8,128]{1,0:T(8,128)S(1)}, f32[8,128]{1,0:T(8,128)S(1)}, u32[]{:S(2)}, u32[]{:S(2)}) collective-permute-start(f32[8,128]{1,0:T(8,128)S(1)} %add_add_fusion.1), channel_id=1, source_target_pairs={{0,128},{64,192},{128,0},{192,64},{1,129},{65,193},{129,1},{193,65... | collective-permute-start | bytes 12296 | tf_op jit(solution)/shard_map/ppermute | solution.py:43
  105.2 3.6 %collective-permute-start.4 = (f32[8,128]{1,0:T(8,128)S(1)}, f32[8,128]{1,0:T(8,128)S(1)}, u32[]{:S(2)}, u32[]{:S(2)}) collective-permute-start(f32[8,128]{1,0:T(8,128)S(1)} %add_add_fusion.1), channel_id=1, source_target_pairs={{0,64},{64,0},{128,192},{192,128},{1,65},{65,1},{129,193},{193,129... | collective-permute-start | bytes 12296 | tf_op jit(solution)/shard_map/ppermute | solution.py:43
Sparse Core Ops, SparseCore 0:
  11.1 96.9 all-gather.1
